TPU v7x, 32 devices: a whole 2x2x4 slice. The times are simulated.
32 devices in a mesh: blk: 8 (over y, x, core), pix: 4 (over z).
Axes of the slice: x: 2, y: 2, z: 4, core: 2. Of those that a mesh axis runs over, the one named last changes fastest.
Arguments:
- particles: bfloat16 [4096, 16384], P('blk', 'pix'), may hold values from -10 to 10, as said below
- ctf: bfloat16 [4096, 16384], P('blk', 'pix'), may hold values from -1 to 1
- noise_var: float32 [16384], P('pix'), may hold values from 0.5 to 4
- projections: bfloat16 [128, 16384], P('blk', 'pix'), may hold values from -3.1 to 3.1
- orient_class: int32 [128], replicated, may hold values from 0 to 4
- class_prior: float32 [5], replicated, may hold values from -2 to 0
- counts: int32 [8], P('blk'), may hold values from 32 to 512, as said below
Outputs:
- class_field: float32 [128, 16384], P('blk', 'pix')
- normalizer: float32 [4096], P('blk')
Inputs may be any that keep to these rules, and one draw needn't show every extreme that they name: `particles`: real values of particle images. Live slots of each index of blk are its first counts slots; some index of blk is full in every draw.
All inputs are finite; a program needn't handle non-finite values.
Results may differ from a plain program's by a relative error of at most 0.0066.
Values may be sent and summed in bfloat16 or wider, within the bound.
No kernel may reach another device: no remote copies, remote signals or barrier semaphores. Data moves between devices by JAX's collectives and lax.ppermute only.
A program may use at most 128 MiB of HBM per device.

v0:
```python
import functools

import jax
import jax.numpy as jnp
from jax import lax
from jax.experimental import pallas as pl
from jax.experimental.pallas import tpu as pltpu
from jax.sharding import PartitionSpec as P


BF16 = jnp.bfloat16
F32 = jnp.float32
MIB = 1 << 20
VMEM = pl.BlockSpec(memory_space=pltpu.VMEM)
SMEM = pl.BlockSpec(memory_space=pltpu.SMEM)
HBM = pl.BlockSpec(memory_space=pltpu.HBM)


def swap(value, axis, size, k):
    out = lax.ppermute(value, axis, [(i, i ^ k) for i in range(size)])
    return pltpu.with_memory_space_constraint(out, pltpu.VMEM)


def params(mib):
    return pltpu.CompilerParams(vmem_limit_bytes=mib * MIB)


def cost(flops, moved):
    return pl.CostEstimate(flops=int(flops), bytes_accessed=int(moved), transcendentals=0)


def prepare_kernel(order, rows, particles, ctf, noise, orient_class, class_prior, weighted, quadratic, prior, *scratch):
    p_buf, c_buf, n_buf, o_buf, r_buf, p_sem, c_sem, small_sem = scratch
    steps, tall, _ = p_buf.shape
    small = []
    for i, (source, target) in enumerate(((noise, n_buf), (orient_class, o_buf), (class_prior, r_buf))):
        small.append(pltpu.make_async_copy(source, target, small_sem.at[i]))
        small[-1].start()
    loads = []
    for s in range(steps):
        span = pl.ds(s * tall, tall)
        a = pltpu.make_async_copy(particles.at[span], p_buf.at[s], p_sem.at[s])
        b = pltpu.make_async_copy(ctf.at[span], c_buf.at[s], c_sem.at[s])
        loads.append((a, b))
    ahead = min(4, steps)
    for a, b in loads[:ahead]:
        a.start()
        b.start()
    for copy in small:
        copy.wait()
    inverse = 1.0 / n_buf[...]
    orients = prior.shape[0]
    me = lax.axis_index("blk")
    classes = o_buf[...]
    table = jnp.zeros(classes.shape, F32)
    for c in range(r_buf.shape[1]):
        table = table + jnp.where(classes == c, r_buf[0:1, c : c + 1], jnp.float32(0.0))
    column = lax.broadcasted_iota(jnp.int32, (rows, orients), 1)
    row = lax.broadcasted_iota(jnp.int32, (rows, orients), 0)
    for slot, k in enumerate(order):
        hit = column == (me ^ k) * rows + row
        picked = jnp.sum(jnp.where(hit, table, jnp.float32(0.0)), axis=1, keepdims=True)
        prior[slot * rows : (slot + 1) * rows, :] = jnp.broadcast_to(picked, (rows, prior.shape[1]))
    for s, (a, b) in enumerate(loads):
        a.wait()
        b.wait()
        if s + ahead < steps:
            for copy in loads[s + ahead]:
                copy.start()
        span = slice(s * tall, (s + 1) * tall)
        wide = c_buf[s].astype(F32)
        scaled = wide * inverse
        weighted[span, :] = (p_buf[s].astype(F32) * scaled).astype(BF16)
        quadratic[span, :] = (wide * scaled).astype(BF16)


def prepare(order, rows, parts, particles, ctf, noise, orient_class, class_prior):
    slots, pixels = particles.shape
    steps = 8 if slots % 128 == 0 else 1
    orients = orient_class.shape[1]
    operands = (particles, ctf, noise, orient_class, class_prior)
    return pl.pallas_call(
        functools.partial(prepare_kernel, order, rows),
        out_shape=(
            pltpu.VMEM((slots, pixels), BF16),
            pltpu.VMEM((slots, pixels), BF16),
            pltpu.VMEM((orients, slots // parts), F32),
        ),
        in_specs=[HBM] * 5,
        out_specs=(VMEM, VMEM, VMEM),
        scratch_shapes=[
            pltpu.VMEM((steps, slots // steps, pixels), BF16),
            pltpu.VMEM((steps, slots // steps, pixels), BF16),
            pltpu.VMEM((1, pixels), F32),
            pltpu.VMEM((1, orients), jnp.int32),
            pltpu.VMEM((1, class_prior.shape[1]), F32),
            pltpu.SemaphoreType.DMA((steps,)),
            pltpu.SemaphoreType.DMA((steps,)),
            pltpu.SemaphoreType.DMA((3,)),
        ],
        compiler_params=params(14),
        cost_estimate=cost(16 * slots * pixels, 8 * slots * pixels),
        name="prepare",
    )(*(pltpu.with_memory_space_constraint(value, pltpu.HBM) for value in operands))


def square_kernel(*refs):
    lines, square = refs[-2:]
    rows = refs[0].shape[0]
    for i, piece in enumerate(refs[:-2]):
        value = piece[...]
        wide = value.astype(F32)
        lines[i * rows : (i + 1) * rows, :] = value
        square[i * rows : (i + 1) * rows, :] = (-0.5 * wide * wide).astype(BF16)


def squares(proj):
    rows, pixels = proj[0].shape
    out = pltpu.VMEM((rows * len(proj), pixels), BF16)
    return pl.pallas_call(
        square_kernel,
        out_shape=(out, out),
        in_specs=[VMEM] * len(proj),
        out_specs=(VMEM, VMEM),
        compiler_params=params(4),
        cost_estimate=cost(1000 * rows * len(proj) * pixels, 6 * rows * len(proj) * pixels),
        name="squares",
    )(*proj)


NT = (((1,), (1,)), ((), ()))


def score_kernel(pieces, parts, *refs):
    proj = refs[:pieces]
    lines, square, weighted, quadratic = refs[pieces : pieces + 4]
    outs = refs[pieces + 4 : pieces + 4 + parts]
    lines_all, square_all, total = refs[pieces + 4 + parts :]
    rows = proj[0].shape[0]
    first = lines.shape[0]
    lines_all[:first, :] = lines[...]
    square_all[:first, :] = square[...]
    for i, piece in enumerate(proj):
        value = piece[...]
        wide = value.astype(F32)
        span = slice(first + i * rows, first + (i + 1) * rows)
        lines_all[span, :] = value
        square_all[span, :] = (-0.5 * wide * wide).astype(BF16)
    total[...] = lax.dot_general(weighted[...], lines_all[...], NT, preferred_element_type=F32) + lax.dot_general(
        quadratic[...], square_all[...], NT, preferred_element_type=F32
    )
    quarter = lax.axis_index("pix")
    lanes = outs[0].shape[1]
    for j, out in enumerate(outs):
        start = pl.multiple_of((quarter ^ j) * lanes, lanes)
        out[...] = total[pl.ds(start, lanes), :].T


def score(parts, proj, lines, square, weighted, quadratic):
    rows, pixels = proj[0].shape
    orients = rows * len(proj) + lines.shape[0]
    slots = weighted.shape[0]
    return pl.pallas_call(
        functools.partial(score_kernel, len(proj), parts),
        out_shape=tuple(pltpu.VMEM((orients, slots // parts), F32) for _ in range(parts)),
        in_specs=[VMEM] * (len(proj) + 4),
        out_specs=(VMEM,) * parts,
        scratch_shapes=[
            pltpu.VMEM((orients, pixels), BF16),
            pltpu.VMEM((orients, pixels), BF16),
            pltpu.VMEM((slots, orients), F32),
        ],
        compiler_params=params(28),
        cost_estimate=cost(4 * orients * slots * pixels, 4 * slots * pixels),
        name="score",
    )(*proj, lines, square, weighted, quadratic)


def weigh_kernel(parts, *refs):
    prior, counts = refs[parts : parts + 2]
    out = refs[parts + 2]
    logits = refs[0][...]
    for piece in refs[1:parts]:
        logits = logits + piece[...]
    logits = logits + prior[...]
    orients, lanes = logits.shape
    peak = jnp.max(logits, axis=0, keepdims=True)
    log_total = peak + jnp.log(jnp.sum(jnp.exp(logits - peak), axis=0, keepdims=True))
    slot = lax.axis_index("pix") * lanes + lax.broadcasted_iota(jnp.int32, (1, lanes), 1)
    live = slot < counts[0]
    out[:orients, :] = jnp.where(live, jnp.exp(logits - log_total), jnp.float32(0.0)).astype(BF16)
    norm = jnp.where(live, log_total, jnp.float32(0.0))
    high = norm.astype(BF16).astype(F32)
    rest = norm - high
    middle = rest.astype(BF16).astype(F32)
    low = rest - middle
    line = lax.broadcasted_iota(jnp.int32, (16, lanes), 0)
    tail = jnp.where(line == 0, high, jnp.where(line == 1, middle, jnp.where(line == 2, low, jnp.float32(0.0))))
    out[orients:, :] = tail.astype(BF16)


def weigh(pieces, prior, counts):
    orients, lanes = prior.shape
    return pl.pallas_call(
        functools.partial(weigh_kernel, len(pieces)),
        out_shape=pltpu.VMEM((orients + 16, lanes), BF16),
        in_specs=[VMEM] * (len(pieces) + 1) + [SMEM],
        out_specs=VMEM,
        compiler_params=params(8),
        cost_estimate=cost(40 * orients * lanes, 20 * orients * lanes),
        name="weigh",
    )(*pieces, prior, counts)


def field_kernel(parts, *refs):
    pieces = refs[:parts]
    weighted, kept, sent, norm, lhs = refs[parts:]
    orients, slots = lhs.shape
    lanes = slots // parts
    quarter = lax.axis_index("pix")
    for j, piece in enumerate(pieces):
        place = quarter ^ j
        start = pl.multiple_of(place * lanes, lanes)
        lhs[:, pl.ds(start, lanes)] = piece[:orients, :]
        tail = piece[orients:, :].astype(F32)
        norm[pl.ds(place, 1), :] = (tail[0:1] + tail[1:2]) + tail[2:3]
    half = orients // 2
    pixels = weighted.shape[1]
    wide = 1024 if pixels % 1024 == 0 else pixels
    for c in range(pixels // wide):
        span = slice(c * wide, (c + 1) * wide)
        value = jnp.dot(lhs[...], weighted[:, span], preferred_element_type=F32)
        kept[:, span] = value[:half]
        sent[:, span] = value[half:].astype(BF16)


def field(pieces, weighted):
    slots, pixels = weighted.shape
    parts = len(pieces)
    orients = pieces[0].shape[0] - 16
    return pl.pallas_call(
        functools.partial(field_kernel, parts),
        out_shape=(
            pltpu.VMEM((orients // 2, pixels), F32),
            pltpu.VMEM((orients // 2, pixels), BF16),
            pltpu.VMEM((parts, slots // parts), F32),
        ),
        in_specs=[VMEM] * (parts + 1),
        out_specs=(VMEM, VMEM, VMEM),
        scratch_shapes=[pltpu.VMEM((orients, slots), BF16)],
        compiler_params=params(16),
        cost_estimate=cost(2 * orients * slots * pixels, 2 * slots * pixels),
        name="field",
    )(*pieces, weighted)


def pair_kernel(kept, got, own, *outs):
    rows = own.shape[0]
    own[...] = kept[:rows, :] + got[:rows, :].astype(F32)
    for i, out in enumerate(outs):
        span = slice((i + 1) * rows, (i + 2) * rows)
        out[...] = (kept[span, :] + got[span, :].astype(F32)).astype(BF16)


def pair(kept, got, rows):
    orients, pixels = kept.shape
    return pl.pallas_call(
        pair_kernel,
        out_shape=(pltpu.VMEM((rows, pixels), F32),) + tuple(pltpu.VMEM((rows, pixels), BF16) for _ in range(orients // rows - 1)),
        in_specs=[VMEM, VMEM],
        out_specs=(VMEM,) * (orients // rows),
        compiler_params=params(8),
        cost_estimate=cost(2 * orients * pixels, 8 * orients * pixels),
        name="pair",
    )(kept, got)


def final_kernel(own, *refs):
    total = own[...]
    for piece in refs[:-1]:
        total = total + piece[...].astype(F32)
    refs[-1][...] = total


def final(own, pieces):
    return pl.pallas_call(
        final_kernel,
        out_shape=jax.ShapeDtypeStruct(own.shape, F32),
        in_specs=[VMEM] * (len(pieces) + 1),
        out_specs=VMEM,
        compiler_params=params(16),
        cost_estimate=cost(own.size * len(pieces), 4 * own.size * len(pieces)),
        name="final",
    )(own, *pieces)


def body(blk, pix, particles, ctf, noise_var, projections, orient_class, class_prior, counts):
    rows = projections.shape[0]
    even = list(range(2, blk, 2))
    order = [0] + even + [k ^ 1 for k in [0] + even]
    noise, orient_class, class_prior = (value.reshape(1, -1) for value in (noise_var, orient_class, class_prior))
    far = {}
    for k in even:
        far[k] = swap(projections, "blk", blk, k)
    near = [swap(projections, "blk", blk, 1)]
    weighted, quadratic, prior = prepare(order, rows, pix, particles, ctf, noise, orient_class, class_prior)
    for k in even:
        near.append(swap(far[k], "blk", blk, 1))
    lines, square = squares([projections] + [far[k] for k in even])
    chunks = score(pix, near, lines, square, weighted, quadratic)
    pieces = [chunks[0]]
    for j in range(1, pix):
        pieces.append(swap(chunks[j], "pix", pix, j))
    weights = weigh(pieces, prior, counts)
    parts = [weights]
    for j in range(1, pix):
        parts.append(swap(weights, "pix", pix, j))
    kept, sent, norm = field(parts, weighted)
    own, *out = pair(kept, swap(sent, "blk", blk, 1), rows)
    got = []
    for piece, k in zip(out, even):
        got.append(swap(piece, "blk", blk, k))
    return final(own, got), norm.reshape(-1)


def solution(mesh):
    placed = (P("blk", "pix"), P("blk", "pix"), P("pix"), P("blk", "pix"), P(), P(), P("blk"))
    return jax.shard_map(
        functools.partial(body, mesh.shape["blk"], mesh.shape["pix"]),
        mesh=mesh,
        in_specs=placed,
        out_specs=(P("blk", "pix"), P("blk")),
        check_vma=False,
    )
```

profile of v0, /device:TPU:0, one launch (start us, length us, event | category | flops | bytes accessed | tf_op | source)
XLA Modules:
  0.0 51.1 jit_solution(5433774783876289842)
XLA Ops:
  0.6 3.0 %collective-permute-start.1 = (bf16[16,4096]{1,0:T(8,128)(2,1)}, bf16[16,4096]{1,0:T(8,128)(2,1)S(1)}, u32[]{:S(2)}, u32[]{:S(2)}) collective-permute-start(bf16[16,4096]{1,0:T(8,128)(2,1)} %refs_0_.1), channel_id=1, source_target_pairs={{0,8},{4,12},{8,0},{12,4},{16,24},{20,28},{24,16},{28,20},{1,9},{5... | collective-permute-start | bytes 393224 | tf_op jit(solution)/shard_map/ppermute | solution.py:20
  3.7 1.5 %collective-permute-start.3 = (bf16[16,4096]{1,0:T(8,128)(2,1)}, bf16[16,4096]{1,0:T(8,128)(2,1)S(1)}, u32[]{:S(2)}, u32[]{:S(2)}) collective-permute-start(bf16[16,4096]{1,0:T(8,128)(2,1)} %refs_0_.1), channel_id=1, source_target_pairs={{0,16},{4,20},{8,24},{12,28},{16,0},{20,4},{24,8},{28,12},{1,17},{... | collective-permute-start | bytes 393224 | tf_op jit(solution)/shard_map/ppermute | solution.py:20
  5.2 2.7 %collective-permute-done.1.refs_1_ = bf16[16,4096]{1,0:T(8,128)(2,1)S(1)} collective-permute-done((bf16[16,4096]{1,0:T(8,128)(2,1)}, bf16[16,4096]{1,0:T(8,128)(2,1)S(1)}, u32[]{:S(2)}, u32[]{:S(2)}) %collective-permute-start.1) | collective-permute-done | bytes 131104 | tf_op jit(solution)/shard_map/ppermute | solution.py:20
  7.9 3.8 %collective-permute-done.3.refs_2_ = bf16[16,4096]{1,0:T(8,128)(2,1)S(1)} collective-permute-done((bf16[16,4096]{1,0:T(8,128)(2,1)}, bf16[16,4096]{1,0:T(8,128)(2,1)S(1)}, u32[]{:S(2)}, u32[]{:S(2)}) %collective-permute-start.3) | collective-permute-done | bytes 131104 | tf_op jit(solution)/shard_map/ppermute | solution.py:20
  12.2 4.6 %prepare.1 = (bf16[512,4096]{1,0:T(8,128)(2,1)S(1)}, bf16[512,4096]{1,0:T(8,128)(2,1)S(1)}, f32[128,128]{1,0:T(8,128)S(1)}) custom-call(bf16[512,4096]{1,0:T(8,128)(2,1)} %particles.1, bf16[512,4096]{1,0:T(8,128)(2,1)} %ctf.1, f32[1,4096]{1,0:T(1,128)} %bitcast.5, s32[1,128]{1,0:T(1,128)} %bitcast.6, f32[1,5]{1,0:T(1,128)} %bitcast.7), custom_call_target="tpu_custom_call" | custom-call | flops 33554432 | bytes 16777216 | tf_op jit(solution)/shard_map/prepare/pallas_call | solution.py:82
  17.0 2.5 %score.1 = (f32[128,128]{1,0:T(8,128)S(1)}, f32[128,128]{1,0:T(8,128)S(1)}, f32[128,128]{1,0:T(8,128)S(1)}, f32[128,128]{1,0:T(8,128)S(1)}) custom-call(bf16[16,4096]{1,0:T(8,128)(2,1)S(1)} %collective-permute-done.refs_0_, bf16[16,4096]{1,0:T(8,128)(2,1)S(1)} %collective-permute-done.2.refs_1_, bf16[16,4096]{1,0:T(8,128)(2,1)S(1)} %collective-permute-done.4.refs_2_, ...), custom_call_target="tpu_custom_call" | custom-call | flops 1073741824 | bytes 8388608 | tf_op jit(solution)/shard_map/score/pallas_call | solution.py:163
  19.4 1.6 %collective-permute-start.7 = (f32[128,128]{1,0:T(8,128)S(1)}, f32[128,128]{1,0:T(8,128)S(1)}, u32[]{:S(2)}, u32[]{:S(2)}) collective-permute-start(f32[128,128]{1,0:T(8,128)S(1)} %get-tuple-element.23), channel_id=1, source_target_pairs={{0,1},{1,0},{2,3},{3,2},{4,5},{5,4},{6,7},{7,6},{8,9},{9,8},{10,11... | collective-permute-start | bytes 196616 | tf_op jit(solution)/shard_map/ppermute | solution.py:20
  21.1 2.6 %collective-permute-start.8 = (f32[128,128]{1,0:T(8,128)S(1)}, f32[128,128]{1,0:T(8,128)S(1)}, u32[]{:S(2)}, u32[]{:S(2)}) collective-permute-start(f32[128,128]{1,0:T(8,128)S(1)} %get-tuple-element.24), channel_id=1, source_target_pairs={{0,2},{1,3},{2,0},{3,1},{4,6},{5,7},{6,4},{7,5},{8,10},{9,11},{10,... | collective-permute-start | bytes 196616 | tf_op jit(solution)/shard_map/ppermute | solution.py:20
  24.5 4.0 %collective-permute-done.8.refs_2_ = f32[128,128]{1,0:T(8,128)S(1)} collective-permute-done((f32[128,128]{1,0:T(8,128)S(1)}, f32[128,128]{1,0:T(8,128)S(1)}, u32[]{:S(2)}, u32[]{:S(2)}) %collective-permute-start.8) | collective-permute-done | bytes 65568 | tf_op jit(solution)/shard_map/ppermute | solution.py:20
  28.5 1.3 %collective-permute-done.9.refs_3_ = f32[128,128]{1,0:T(8,128)S(1)} collective-permute-done((f32[128,128]{1,0:T(8,128)S(1)}, f32[128,128]{1,0:T(8,128)S(1)}, u32[]{:S(2)}, u32[]{:S(2)}) %collective-permute-start.9) | collective-permute-done | bytes 65568 | tf_op jit(solution)/shard_map/ppermute | solution.py:20
  29.9 0.8 %collective-permute-start.10 = (bf16[144,128]{1,0:T(8,128)(2,1)S(1)}, bf16[144,128]{1,0:T(8,128)(2,1)S(1)}, u32[]{:S(2)}, u32[]{:S(2)}) collective-permute-start(bf16[144,128]{1,0:T(8,128)(2,1)S(1)} %weigh.1.refs_0_), channel_id=1, source_target_pairs={{0,1},{1,0},{2,3},{3,2},{4,5},{5,4},{6,7},{7,6},{8,9},{9,8},{10,11... | collective-permute-start | bytes 110600 | tf_op jit(solution)/shard_map/ppermute | solution.py:20
  30.7 1.7 %collective-permute-start.11 = (bf16[144,128]{1,0:T(8,128)(2,1)S(1)}, bf16[144,128]{1,0:T(8,128)(2,1)S(1)}, u32[]{:S(2)}, u32[]{:S(2)}) collective-permute-start(bf16[144,128]{1,0:T(8,128)(2,1)S(1)} %weigh.1.refs_0_), channel_id=1, source_target_pairs={{0,2},{1,3},{2,0},{3,1},{4,6},{5,7},{6,4},{7,5},{8,10},{9,11},{10,... | collective-permute-start | bytes 110600 | tf_op jit(solution)/shard_map/ppermute | solution.py:20
  32.4 2.0 %collective-permute-start.12 = (bf16[144,128]{1,0:T(8,128)(2,1)S(1)}, bf16[144,128]{1,0:T(8,128)(2,1)S(1)}, u32[]{:S(2)}, u32[]{:S(2)}) collective-permute-start(bf16[144,128]{1,0:T(8,128)(2,1)S(1)} %weigh.1.refs_0_), channel_id=1, source_target_pairs={{0,3},{1,2},{2,1},{3,0},{4,7},{5,6},{6,5},{7,4},{8,11},{9,10},{10,... | collective-permute-start | bytes 110600 | tf_op jit(solution)/shard_map/ppermute | solution.py:20
  34.4 1.2 %collective-permute-done.11.refs_2_ = bf16[144,128]{1,0:T(8,128)(2,1)S(1)} collective-permute-done((bf16[144,128]{1,0:T(8,128)(2,1)S(1)}, bf16[144,128]{1,0:T(8,128)(2,1)S(1)}, u32[]{:S(2)}, u32[]{:S(2)}) %collective-permute-start.11) | collective-permute-done | bytes 36896 | tf_op jit(solution)/shard_map/ppermute | solution.py:20
  35.6 2.6 %collective-permute-done.12.refs_3_ = bf16[144,128]{1,0:T(8,128)(2,1)S(1)} collective-permute-done((bf16[144,128]{1,0:T(8,128)(2,1)S(1)}, bf16[144,128]{1,0:T(8,128)(2,1)S(1)}, u32[]{:S(2)}, u32[]{:S(2)}) %collective-permute-start.12) | collective-permute-done | bytes 36896 | tf_op jit(solution)/shard_map/ppermute | solution.py:20
  38.1 0.7 %field.1 = (f32[64,4096]{1,0:T(8,128)S(1)}, bf16[64,4096]{1,0:T(8,128)(2,1)S(1)}, f32[4,128]{1,0:T(4,128)S(1)}) custom-call(bf16[144,128]{1,0:T(8,128)(2,1)S(1)} %weigh.1.refs_0_, bf16[144,128]{1,0:T(8,128)(2,1)S(1)} %collective-permute-done.10.refs_1_, bf16[144,128]{1,0:T(8,128)(2,1)S(1)} %collective-permute-done.11.refs_2_, ...), custom_call_target="tpu_custom_call" | custom-call | flops 536870912 | bytes 4194304 | tf_op jit(solution)/shard_map/field/pallas_call | solution.py:241
  39.0 1.9 %collective-permute-done.13.got = bf16[64,4096]{1,0:T(8,128)(2,1)S(1)} collective-permute-done((bf16[64,4096]{1,0:T(8,128)(2,1)S(1)}, bf16[64,4096]{1,0:T(8,128)(2,1)S(1)}, u32[]{:S(2)}, u32[]{:S(2)}) %collective-permute-start.13) | collective-permute-done | bytes 524320 | tf_op jit(solution)/shard_map/ppermute | solution.py:20
  40.9 1.3 %collective-permute-start.14 = (bf16[16,4096]{1,0:T(8,128)(2,1)S(1)}, bf16[16,4096]{1,0:T(8,128)(2,1)S(1)}, u32[]{:S(2)}, u32[]{:S(2)}) collective-permute-start(bf16[16,4096]{1,0:T(8,128)(2,1)S(1)} %get-tuple-element.30), channel_id=1, source_target_pairs={{0,8},{4,12},{8,0},{12,4},{16,24},{20,28},{24,16},{28,20},{1,9},{5... | collective-permute-start | bytes 393224 | tf_op jit(solution)/shard_map/ppermute | solution.py:20
  42.2 0.8 %collective-permute-start.15 = (bf16[16,4096]{1,0:T(8,128)(2,1)S(1)}, bf16[16,4096]{1,0:T(8,128)(2,1)S(1)}, u32[]{:S(2)}, u32[]{:S(2)}) collective-permute-start(bf16[16,4096]{1,0:T(8,128)(2,1)S(1)} %get-tuple-element.31), channel_id=1, source_target_pairs={{0,16},{4,20},{8,24},{12,28},{16,0},{20,4},{24,8},{28,12},{1,17},{... | collective-permute-start | bytes 393224 | tf_op jit(solution)/shard_map/ppermute | solution.py:20
  43.1 1.4 %collective-permute-start.16 = (bf16[16,4096]{1,0:T(8,128)(2,1)S(1)}, bf16[16,4096]{1,0:T(8,128)(2,1)S(1)}, u32[]{:S(2)}, u32[]{:S(2)}) collective-permute-start(bf16[16,4096]{1,0:T(8,128)(2,1)S(1)} %get-tuple-element.32), channel_id=1, source_target_pairs={{0,24},{4,28},{8,16},{12,20},{16,8},{20,12},{24,0},{28,4},{1,25},{... | collective-permute-start | bytes 393224 | tf_op jit(solution)/shard_map/ppermute | solution.py:20
  45.1 2.2 %collective-permute-done.14.refs_0_ = bf16[16,4096]{1,0:T(8,128)(2,1)S(1)} collective-permute-done((bf16[16,4096]{1,0:T(8,128)(2,1)S(1)}, bf16[16,4096]{1,0:T(8,128)(2,1)S(1)}, u32[]{:S(2)}, u32[]{:S(2)}) %collective-permute-start.14) | collective-permute-done | bytes 131104 | tf_op jit(solution)/shard_map/ppermute | solution.py:20
  47.2 1.4 %collective-permute-done.15.refs_1_ = bf16[16,4096]{1,0:T(8,128)(2,1)S(1)} collective-permute-done((bf16[16,4096]{1,0:T(8,128)(2,1)S(1)}, bf16[16,4096]{1,0:T(8,128)(2,1)S(1)}, u32[]{:S(2)}, u32[]{:S(2)}) %collective-permute-start.15) | collective-permute-done | bytes 131104 | tf_op jit(solution)/shard_map/ppermute | solution.py:20
  48.7 1.6 %collective-permute-done.16.refs_2_ = bf16[16,4096]{1,0:T(8,128)(2,1)S(1)} collective-permute-done((bf16[16,4096]{1,0:T(8,128)(2,1)S(1)}, bf16[16,4096]{1,0:T(8,128)(2,1)S(1)}, u32[]{:S(2)}, u32[]{:S(2)}) %collective-permute-start.16) | collective-permute-done | bytes 131104 | tf_op jit(solution)/shard_map/ppermute | solution.py:20
  50.3 0.8 %final.1 = f32[16,4096]{1,0:T(8,128)} custom-call(f32[16,4096]{1,0:T(8,128)S(1)} %get-tuple-element.29.own, bf16[16,4096]{1,0:T(8,128)(2,1)S(1)} %collective-permute-done.14.refs_0_, bf16[16,4096]{1,0:T(8,128)(2,1)S(1)} %collective-permute-done.15.refs_1_, bf16[16,4096]{1,0:T(8,128)(2,1)S(1)} %collective-permute-done.16.refs_2_), custom_call_target="tpu_custom_call" | custom-call | flops 196608 | bytes 786432 | tf_op jit(solution)/shard_map/final/pallas_call | solution.py:286
  (20 shorter events, 1.8 us)
Async XLA Ops:
  0.6 7.2 %collective-permute-start.1 = (bf16[16,4096]{1,0:T(8,128)(2,1)}, bf16[16,4096]{1,0:T(8,128)(2,1)S(1)}, u32[]{:S(2)}, u32[]{:S(2)}) collective-permute-start(bf16[16,4096]{1,0:T(8,128)(2,1)} %refs_0_.1), channel_id=1, source_target_pairs={{0,8},{4,12},{8,0},{12,4},{16,24},{20,28},{24,16},{28,20},{1,9},{5... | collective-permute-start | bytes 393224 | tf_op jit(solution)/shard_map/ppermute | solution.py:20
  3.7 8.0 %collective-permute-start.3 = (bf16[16,4096]{1,0:T(8,128)(2,1)}, bf16[16,4096]{1,0:T(8,128)(2,1)S(1)}, u32[]{:S(2)}, u32[]{:S(2)}) collective-permute-start(bf16[16,4096]{1,0:T(8,128)(2,1)} %refs_0_.1), channel_id=1, source_target_pairs={{0,16},{4,20},{8,24},{12,28},{16,0},{20,4},{24,8},{28,12},{1,17},{... | collective-permute-start | bytes 393224 | tf_op jit(solution)/shard_map/ppermute | solution.py:20
  5.2 6.5 %collective-permute-start.5 = (bf16[16,4096]{1,0:T(8,128)(2,1)}, bf16[16,4096]{1,0:T(8,128)(2,1)S(1)}, u32[]{:S(2)}, u32[]{:S(2)}) collective-permute-start(bf16[16,4096]{1,0:T(8,128)(2,1)} %refs_0_.1), channel_id=1, source_target_pairs={{0,24},{4,28},{8,16},{12,20},{16,8},{20,12},{24,0},{28,4},{1,25},{... | collective-permute-start | bytes 393224 | tf_op jit(solution)/shard_map/ppermute | solution.py:20
  5.2 11.7 %collective-permute-start = (bf16[16,4096]{1,0:T(8,128)(2,1)}, bf16[16,4096]{1,0:T(8,128)(2,1)S(1)}, u32[]{:S(2)}, u32[]{:S(2)}) collective-permute-start(bf16[16,4096]{1,0:T(8,128)(2,1)} %refs_0_.1), channel_id=1, source_target_pairs={{0,4},{4,0},{8,12},{12,8},{16,20},{20,16},{24,28},{28,24},{1,5},{5... | collective-permute-start | bytes 393224 | tf_op jit(solution)/shard_map/ppermute | solution.py:20
  7.9 9.1 %collective-permute-start.2 = (bf16[16,4096]{1,0:T(8,128)(2,1)S(1)}, bf16[16,4096]{1,0:T(8,128)(2,1)S(1)}, u32[]{:S(2)}, u32[]{:S(2)}) collective-permute-start(bf16[16,4096]{1,0:T(8,128)(2,1)S(1)} %collective-permute-done.1.refs_1_), channel_id=1, source_target_pairs={{0,4},{4,0},{8,12},{12,8},{16,20},{20,16},{24,28},{28,24},{1,5},{5... | collective-permute-start | bytes 393224 | tf_op jit(solution)/shard_map/ppermute | solution.py:20
  11.7 5.3 %collective-permute-start.4 = (bf16[16,4096]{1,0:T(8,128)(2,1)S(1)}, bf16[16,4096]{1,0:T(8,128)(2,1)S(1)}, u32[]{:S(2)}, u32[]{:S(2)}) collective-permute-start(bf16[16,4096]{1,0:T(8,128)(2,1)S(1)} %collective-permute-done.3.refs_2_), channel_id=1, source_target_pairs={{0,4},{4,0},{8,12},{12,8},{16,20},{20,16},{24,28},{28,24},{1,5},{5... | collective-permute-start | bytes 393224 | tf_op jit(solution)/shard_map/ppermute | solution.py:20
  11.7 5.3 %collective-permute-start.6 = (bf16[16,4096]{1,0:T(8,128)(2,1)S(1)}, bf16[16,4096]{1,0:T(8,128)(2,1)S(1)}, u32[]{:S(2)}, u32[]{:S(2)}) collective-permute-start(bf16[16,4096]{1,0:T(8,128)(2,1)S(1)} %collective-permute-done.5.refs_3_), channel_id=1, source_target_pairs={{0,4},{4,0},{8,12},{12,8},{16,20},{20,16},{24,28},{28,24},{1,5},{5... | collective-permute-start | bytes 393224 | tf_op jit(solution)/shard_map/ppermute | solution.py:20
  12.2 4.6 %copy-start = (bf16[16,4096]{1,0:T(8,128)(2,1)S(1)}, bf16[16,4096]{1,0:T(8,128)(2,1)}, u32[]{:S(2)}) copy-start(bf16[16,4096]{1,0:T(8,128)(2,1)} %refs_0_.1) | copy-start | bytes 393220
  19.4 5.1 %collective-permute-start.7 = (f32[128,128]{1,0:T(8,128)S(1)}, f32[128,128]{1,0:T(8,128)S(1)}, u32[]{:S(2)}, u32[]{:S(2)}) collective-permute-start(f32[128,128]{1,0:T(8,128)S(1)} %get-tuple-element.23), channel_id=1, source_target_pairs={{0,1},{1,0},{2,3},{3,2},{4,5},{5,4},{6,7},{7,6},{8,9},{9,8},{10,11... | collective-permute-start | bytes 196616 | tf_op jit(solution)/shard_map/ppermute | solution.py:20
  21.1 7.5 %collective-permute-start.8 = (f32[128,128]{1,0:T(8,128)S(1)}, f32[128,128]{1,0:T(8,128)S(1)}, u32[]{:S(2)}, u32[]{:S(2)}) collective-permute-start(f32[128,128]{1,0:T(8,128)S(1)} %get-tuple-element.24), channel_id=1, source_target_pairs={{0,2},{1,3},{2,0},{3,1},{4,6},{5,7},{6,4},{7,5},{8,10},{9,11},{10,... | collective-permute-start | bytes 196616 | tf_op jit(solution)/shard_map/ppermute | solution.py:20
  23.7 6.2 %collective-permute-start.9 = (f32[128,128]{1,0:T(8,128)S(1)}, f32[128,128]{1,0:T(8,128)S(1)}, u32[]{:S(2)}, u32[]{:S(2)}) collective-permute-start(f32[128,128]{1,0:T(8,128)S(1)} %get-tuple-element.25), channel_id=1, source_target_pairs={{0,3},{1,2},{2,1},{3,0},{4,7},{5,6},{6,5},{7,4},{8,11},{9,10},{10,... | collective-permute-start | bytes 196616 | tf_op jit(solution)/shard_map/ppermute | solution.py:20
  29.9 4.5 %collective-permute-start.10 = (bf16[144,128]{1,0:T(8,128)(2,1)S(1)}, bf16[144,128]{1,0:T(8,128)(2,1)S(1)}, u32[]{:S(2)}, u32[]{:S(2)}) collective-permute-start(bf16[144,128]{1,0:T(8,128)(2,1)S(1)} %weigh.1.refs_0_), channel_id=1, source_target_pairs={{0,1},{1,0},{2,3},{3,2},{4,5},{5,4},{6,7},{7,6},{8,9},{9,8},{10,11... | collective-permute-start | bytes 110600 | tf_op jit(solution)/shard_map/ppermute | solution.py:20
  30.7 4.9 %collective-permute-start.11 = (bf16[144,128]{1,0:T(8,128)(2,1)S(1)}, bf16[144,128]{1,0:T(8,128)(2,1)S(1)}, u32[]{:S(2)}, u32[]{:S(2)}) collective-permute-start(bf16[144,128]{1,0:T(8,128)(2,1)S(1)} %weigh.1.refs_0_), channel_id=1, source_target_pairs={{0,2},{1,3},{2,0},{3,1},{4,6},{5,7},{6,4},{7,5},{8,10},{9,11},{10,... | collective-permute-start | bytes 110600 | tf_op jit(solution)/shard_map/ppermute | solution.py:20
  32.4 5.8 %collective-permute-start.12 = (bf16[144,128]{1,0:T(8,128)(2,1)S(1)}, bf16[144,128]{1,0:T(8,128)(2,1)S(1)}, u32[]{:S(2)}, u32[]{:S(2)}) collective-permute-start(bf16[144,128]{1,0:T(8,128)(2,1)S(1)} %weigh.1.refs_0_), channel_id=1, source_target_pairs={{0,3},{1,2},{2,1},{3,0},{4,7},{5,6},{6,5},{7,4},{8,11},{9,10},{10,... | collective-permute-start | bytes 110600 | tf_op jit(solution)/shard_map/ppermute | solution.py:20
  38.9 2.0 %collective-permute-start.13 = (bf16[64,4096]{1,0:T(8,128)(2,1)S(1)}, bf16[64,4096]{1,0:T(8,128)(2,1)S(1)}, u32[]{:S(2)}, u32[]{:S(2)}) collective-permute-start(bf16[64,4096]{1,0:T(8,128)(2,1)S(1)} %get-tuple-element.28), channel_id=1, source_target_pairs={{0,4},{4,0},{8,12},{12,8},{16,20},{20,16},{24,28},{28,24},{1,5},{5... | collective-permute-start | bytes 1572872 | tf_op jit(solution)/shard_map/ppermute | solution.py:20
  40.9 6.3 %collective-permute-start.14 = (bf16[16,4096]{1,0:T(8,128)(2,1)S(1)}, bf16[16,4096]{1,0:T(8,128)(2,1)S(1)}, u32[]{:S(2)}, u32[]{:S(2)}) collective-permute-start(bf16[16,4096]{1,0:T(8,128)(2,1)S(1)} %get-tuple-element.30), channel_id=1, source_target_pairs={{0,8},{4,12},{8,0},{12,4},{16,24},{20,28},{24,16},{28,20},{1,9},{5... | collective-permute-start | bytes 393224 | tf_op jit(solution)/shard_map/ppermute | solution.py:20
  42.2 6.4 %collective-permute-start.15 = (bf16[16,4096]{1,0:T(8,128)(2,1)S(1)}, bf16[16,4096]{1,0:T(8,128)(2,1)S(1)}, u32[]{:S(2)}, u32[]{:S(2)}) collective-permute-start(bf16[16,4096]{1,0:T(8,128)(2,1)S(1)} %get-tuple-element.31), channel_id=1, source_target_pairs={{0,16},{4,20},{8,24},{12,28},{16,0},{20,4},{24,8},{28,12},{1,17},{... | collective-permute-start | bytes 393224 | tf_op jit(solution)/shard_map/ppermute | solution.py:20
  43.1 7.3 %collective-permute-start.16 = (bf16[16,4096]{1,0:T(8,128)(2,1)S(1)}, bf16[16,4096]{1,0:T(8,128)(2,1)S(1)}, u32[]{:S(2)}, u32[]{:S(2)}) collective-permute-start(bf16[16,4096]{1,0:T(8,128)(2,1)S(1)} %get-tuple-element.32), channel_id=1, source_target_pairs={{0,24},{4,28},{8,16},{12,20},{16,8},{20,12},{24,0},{28,4},{1,25},{... | collective-permute-start | bytes 393224 | tf_op jit(solution)/shard_map/ppermute | solution.py:20
where the time goes:
time: 51.2 us; the launch traced here: 51.1 us
  waiting for transfers between devices  22.6 us (44%)
  starting transfers between devices  17.6 us (34%)
  Pallas kernels  8.82 us (17%)
  between operations  1.4 us (3%)
  local copies, waits for them, and re-layouts  0.58 us (1%)
    ppermute x17, waiting for transfers between devices, swap(): out = lax.ppermute(value, axis, [(i, i ^ k) for i in range(size)])  22.6 us
    ppermute x17, starting transfers between devices, swap(): out = lax.ppermute(value, axis, [(i, i ^ k) for i in range(size)])  17.6 us
    pallas_call x1, Pallas kernels, prepare(): pl.pallas_call(functools.partial(prepare_kernel, order, rows), out_shape=...  4.55 us
    pallas_call x1, Pallas kernels, score(): pl.pallas_call(functools.partial(score_kernel, len(proj), parts), out_sha...  2.46 us
  transfers between devices with their start and end apart: 17, of which 10 were waited for; matrix products, arithmetic and copies ran while one was open for 1% of the time, Pallas kernels for 9%

commit v1 on v0

--- a/solution.py
+++ b/solution.py
@@ -214,7 +214,7 @@
 
 def field_kernel(parts, *refs):
     pieces = refs[:parts]
-    weighted, kept, sent, norm, lhs = refs[parts:]
+    weighted, kept, sent, late, norm, lhs = refs[parts:]
     orients, slots = lhs.shape
     lanes = slots // parts
     quarter = lax.axis_index("pix")
@@ -231,10 +231,12 @@
         span = slice(c * wide, (c + 1) * wide)
         value = jnp.dot(lhs[...], weighted[:, span], preferred_element_type=F32)
         kept[:, span] = value[:half]
-        sent[:, span] = value[half:].astype(BF16)
-
-
-def field(pieces, weighted):
+        rest = value[half:].astype(BF16)
+        sent[:, span] = rest[: sent.shape[0]]
+        late[:, span] = rest[sent.shape[0] :]
+
+
+def field(pieces, weighted, first):
     slots, pixels = weighted.shape
     parts = len(pieces)
     orients = pieces[0].shape[0] - 16
@@ -242,11 +244,12 @@
         functools.partial(field_kernel, parts),
         out_shape=(
             pltpu.VMEM((orients // 2, pixels), F32),
-            pltpu.VMEM((orients // 2, pixels), BF16),
+            pltpu.VMEM((first, pixels), BF16),
+            pltpu.VMEM((orients // 2 - first, pixels), BF16),
             pltpu.VMEM((parts, slots // parts), F32),
         ),
         in_specs=[VMEM] * (parts + 1),
-        out_specs=(VMEM, VMEM, VMEM),
+        out_specs=(VMEM,) * 4,
         scratch_shapes=[pltpu.VMEM((orients, slots), BF16)],
         compiler_params=params(16),
         cost_estimate=cost(2 * orients * slots * pixels, 2 * slots * pixels),
@@ -254,21 +257,21 @@
     )(*pieces, weighted)
 
 
-def pair_kernel(kept, got, own, *outs):
-    rows = own.shape[0]
-    own[...] = kept[:rows, :] + got[:rows, :].astype(F32)
+def pair_kernel(base, kept, got, *outs):
+    rows = outs[0].shape[0]
     for i, out in enumerate(outs):
-        span = slice((i + 1) * rows, (i + 2) * rows)
-        out[...] = (kept[span, :] + got[span, :].astype(F32)).astype(BF16)
-
-
-def pair(kept, got, rows):
-    orients, pixels = kept.shape
-    return pl.pallas_call(
-        pair_kernel,
-        out_shape=(pltpu.VMEM((rows, pixels), F32),) + tuple(pltpu.VMEM((rows, pixels), BF16) for _ in range(orients // rows - 1)),
+        span = slice(i * rows, (i + 1) * rows)
+        mine = slice(base + i * rows, base + (i + 1) * rows)
+        out[...] = (kept[mine, :] + got[span, :].astype(F32)).astype(out.dtype)
+
+
+def pair(kept, got, rows, base, types):
+    orients, pixels = got.shape
+    return pl.pallas_call(
+        functools.partial(pair_kernel, base),
+        out_shape=tuple(pltpu.VMEM((rows, pixels), kind) for kind in types),
         in_specs=[VMEM, VMEM],
-        out_specs=(VMEM,) * (orients // rows),
+        out_specs=(VMEM,) * len(types),
         compiler_params=params(8),
         cost_estimate=cost(2 * orients * pixels, 8 * orients * pixels),
         name="pair",
@@ -297,17 +300,19 @@
 def body(blk, pix, particles, ctf, noise_var, projections, orient_class, class_prior, counts):
     rows = projections.shape[0]
     even = list(range(2, blk, 2))
-    order = [0] + even + [k ^ 1 for k in [0] + even]
+    lead = even[:-1] + [0] + even[-1:]
+    order = lead + [k ^ 1 for k in lead]
     noise, orient_class, class_prior = (value.reshape(1, -1) for value in (noise_var, orient_class, class_prior))
-    far = {}
+    far = {0: projections}
+    near = {}
     for k in even:
         far[k] = swap(projections, "blk", blk, k)
-    near = [swap(projections, "blk", blk, 1)]
+    near[0] = swap(projections, "blk", blk, 1)
     weighted, quadratic, prior = prepare(order, rows, pix, particles, ctf, noise, orient_class, class_prior)
     for k in even:
-        near.append(swap(far[k], "blk", blk, 1))
-    lines, square = squares([projections] + [far[k] for k in even])
-    chunks = score(pix, near, lines, square, weighted, quadratic)
+        near[k] = swap(far[k], "blk", blk, 1)
+    lines, square = squares([far[k] for k in lead])
+    chunks = score(pix, [near[k] for k in lead], lines, square, weighted, quadratic)
     pieces = [chunks[0]]
     for j in range(1, pix):
         pieces.append(swap(chunks[j], "pix", pix, j))
@@ -315,10 +320,14 @@
     parts = [weights]
     for j in range(1, pix):
         parts.append(swap(weights, "pix", pix, j))
-    kept, sent, norm = field(parts, weighted)
-    own, *out = pair(kept, swap(sent, "blk", blk, 1), rows)
+    first = rows * (len(lead) - 2)
+    kept, sent, late, norm = field(parts, weighted, first)
+    sent = swap(sent, "blk", blk, 1)
+    late = swap(late, "blk", blk, 1)
+    out = list(pair(kept, sent, rows, 0, [BF16] * (len(lead) - 2)))
+    own, last = pair(kept, late, rows, first, [F32, BF16])
     got = []
-    for piece, k in zip(out, even):
+    for piece, k in zip(out + [last], even):
         got.append(swap(piece, "blk", blk, k))
     return final(own, got), norm.reshape(-1)
 

time: 51.2 us -> 50.8 us (level)
  waiting for transfers between devices: 22.6 us -> 21.7 us
  starting transfers between devices: 17.6 us -> 18.2 us
    ppermute x17 -> x18, waiting for transfers between devices: 22.6 us -> 21.7 us  [swap(): out = lax.ppermute(value, axis, [(i, i ^ k) for i in range(size)])]
    ppermute x17 -> x18, starting transfers between devices: 17.6 us -> 18.2 us  [swap(): out = lax.ppermute(value, axis, [(i, i ^ k) for i in range(size)])]
  transfers between devices with their start and end apart: 17 -> 18, of which waited for: 10 -> 10; matrix products, arithmetic and copies ran while one was open for 1% -> 1% of each run, Pallas kernels for 9% -> 10%
where the time goes in v1:
time: 50.8 us; the launch traced here: 50.6 us
  waiting for transfers between devices  21.7 us (43%)
  starting transfers between devices  18.2 us (36%)
  Pallas kernels  8.83 us (17%)
  between operations  1.4 us (3%)
  local copies, waits for them, and re-layouts  0.58 us (1%)
    ppermute x18, waiting for transfers between devices, swap(): out = lax.ppermute(value, axis, [(i, i ^ k) for i in range(size)])  21.7 us
    ppermute x18, starting transfers between devices, swap(): out = lax.ppermute(value, axis, [(i, i ^ k) for i in range(size)])  18.2 us
    pallas_call x1, Pallas kernels, prepare(): pl.pallas_call(functools.partial(prepare_kernel, order, rows), out_shape=...  4.55 us
    pallas_call x1, Pallas kernels, score(): pl.pallas_call(functools.partial(score_kernel, len(proj), parts), out_sha...  2.46 us
  transfers between devices with their start and end apart: 18, of which 10 were waited for; matrix products, arithmetic and copies ran while one was open for 1% of the time, Pallas kernels for 10%

profile of v1, /device:TPU:0, one launch (start us, length us, event | category | flops | bytes accessed | tf_op | source)
XLA Modules:
  0.0 50.6 jit_solution(7316314939827228420)
XLA Ops:
  0.6 3.0 %collective-permute-start = (bf16[16,4096]{1,0:T(8,128)(2,1)}, bf16[16,4096]{1,0:T(8,128)(2,1)S(1)}, u32[]{:S(2)}, u32[]{:S(2)}) collective-permute-start(bf16[16,4096]{1,0:T(8,128)(2,1)} %refs_2_.1), channel_id=1, source_target_pairs={{0,8},{4,12},{8,0},{12,4},{16,24},{20,28},{24,16},{28,20},{1,9},{5... | collective-permute-start | bytes 393224 | tf_op jit(solution)/shard_map/ppermute | solution.py:20
  3.7 1.5 %collective-permute-start.2 = (bf16[16,4096]{1,0:T(8,128)(2,1)}, bf16[16,4096]{1,0:T(8,128)(2,1)S(1)}, u32[]{:S(2)}, u32[]{:S(2)}) collective-permute-start(bf16[16,4096]{1,0:T(8,128)(2,1)} %refs_2_.1), channel_id=1, source_target_pairs={{0,16},{4,20},{8,24},{12,28},{16,0},{20,4},{24,8},{28,12},{1,17},{... | collective-permute-start | bytes 393224 | tf_op jit(solution)/shard_map/ppermute | solution.py:20
  5.2 2.7 %collective-permute-done.refs_0_ = bf16[16,4096]{1,0:T(8,128)(2,1)S(1)} collective-permute-done((bf16[16,4096]{1,0:T(8,128)(2,1)}, bf16[16,4096]{1,0:T(8,128)(2,1)S(1)}, u32[]{:S(2)}, u32[]{:S(2)}) %collective-permute-start) | collective-permute-done | bytes 131104 | tf_op jit(solution)/shard_map/ppermute | solution.py:20
  7.9 3.8 %collective-permute-done.2.refs_1_ = bf16[16,4096]{1,0:T(8,128)(2,1)S(1)} collective-permute-done((bf16[16,4096]{1,0:T(8,128)(2,1)}, bf16[16,4096]{1,0:T(8,128)(2,1)S(1)}, u32[]{:S(2)}, u32[]{:S(2)}) %collective-permute-start.2) | collective-permute-done | bytes 131104 | tf_op jit(solution)/shard_map/ppermute | solution.py:20
  12.2 4.6 %prepare.1 = (bf16[512,4096]{1,0:T(8,128)(2,1)S(1)}, bf16[512,4096]{1,0:T(8,128)(2,1)S(1)}, f32[128,128]{1,0:T(8,128)S(1)}) custom-call(bf16[512,4096]{1,0:T(8,128)(2,1)} %particles.1, bf16[512,4096]{1,0:T(8,128)(2,1)} %ctf.1, f32[1,4096]{1,0:T(1,128)} %bitcast.5, s32[1,128]{1,0:T(1,128)} %bitcast.6, f32[1,5]{1,0:T(1,128)} %bitcast.7), custom_call_target="tpu_custom_call" | custom-call | flops 33554432 | bytes 16777216 | tf_op jit(solution)/shard_map/prepare/pallas_call | solution.py:82
  17.0 2.5 %score.1 = (f32[128,128]{1,0:T(8,128)S(1)}, f32[128,128]{1,0:T(8,128)S(1)}, f32[128,128]{1,0:T(8,128)S(1)}, f32[128,128]{1,0:T(8,128)S(1)}) custom-call(bf16[16,4096]{1,0:T(8,128)(2,1)S(1)} %collective-permute-done.1.refs_0_, bf16[16,4096]{1,0:T(8,128)(2,1)S(1)} %collective-permute-done.3.refs_1_, bf16[16,4096]{1,0:T(8,128)(2,1)S(1)} %collective-permute-done.4.refs_2_, ...), custom_call_target="tpu_custom_call" | custom-call | flops 1073741824 | bytes 8388608 | tf_op jit(solution)/shard_map/score/pallas_call | solution.py:163
  19.4 1.6 %collective-permute-start.7 = (f32[128,128]{1,0:T(8,128)S(1)}, f32[128,128]{1,0:T(8,128)S(1)}, u32[]{:S(2)}, u32[]{:S(2)}) collective-permute-start(f32[128,128]{1,0:T(8,128)S(1)} %get-tuple-element.24), channel_id=1, source_target_pairs={{0,1},{1,0},{2,3},{3,2},{4,5},{5,4},{6,7},{7,6},{8,9},{9,8},{10,11... | collective-permute-start | bytes 196616 | tf_op jit(solution)/shard_map/ppermute | solution.py:20
  21.1 2.6 %collective-permute-start.8 = (f32[128,128]{1,0:T(8,128)S(1)}, f32[128,128]{1,0:T(8,128)S(1)}, u32[]{:S(2)}, u32[]{:S(2)}) collective-permute-start(f32[128,128]{1,0:T(8,128)S(1)} %get-tuple-element.25), channel_id=1, source_target_pairs={{0,2},{1,3},{2,0},{3,1},{4,6},{5,7},{6,4},{7,5},{8,10},{9,11},{10,... | collective-permute-start | bytes 196616 | tf_op jit(solution)/shard_map/ppermute | solution.py:20
  24.5 4.0 %collective-permute-done.8.refs_2_ = f32[128,128]{1,0:T(8,128)S(1)} collective-permute-done((f32[128,128]{1,0:T(8,128)S(1)}, f32[128,128]{1,0:T(8,128)S(1)}, u32[]{:S(2)}, u32[]{:S(2)}) %collective-permute-start.8) | collective-permute-done | bytes 65568 | tf_op jit(solution)/shard_map/ppermute | solution.py:20
  28.5 1.3 %collective-permute-done.9.refs_3_ = f32[128,128]{1,0:T(8,128)S(1)} collective-permute-done((f32[128,128]{1,0:T(8,128)S(1)}, f32[128,128]{1,0:T(8,128)S(1)}, u32[]{:S(2)}, u32[]{:S(2)}) %collective-permute-start.9) | collective-permute-done | bytes 65568 | tf_op jit(solution)/shard_map/ppermute | solution.py:20
  29.9 0.8 %collective-permute-start.10 = (bf16[144,128]{1,0:T(8,128)(2,1)S(1)}, bf16[144,128]{1,0:T(8,128)(2,1)S(1)}, u32[]{:S(2)}, u32[]{:S(2)}) collective-permute-start(bf16[144,128]{1,0:T(8,128)(2,1)S(1)} %weigh.1.refs_0_), channel_id=1, source_target_pairs={{0,1},{1,0},{2,3},{3,2},{4,5},{5,4},{6,7},{7,6},{8,9},{9,8},{10,11... | collective-permute-start | bytes 110600 | tf_op jit(solution)/shard_map/ppermute | solution.py:20
  30.7 1.7 %collective-permute-start.11 = (bf16[144,128]{1,0:T(8,128)(2,1)S(1)}, bf16[144,128]{1,0:T(8,128)(2,1)S(1)}, u32[]{:S(2)}, u32[]{:S(2)}) collective-permute-start(bf16[144,128]{1,0:T(8,128)(2,1)S(1)} %weigh.1.refs_0_), channel_id=1, source_target_pairs={{0,2},{1,3},{2,0},{3,1},{4,6},{5,7},{6,4},{7,5},{8,10},{9,11},{10,... | collective-permute-start | bytes 110600 | tf_op jit(solution)/shard_map/ppermute | solution.py:20
  32.4 2.0 %collective-permute-start.12 = (bf16[144,128]{1,0:T(8,128)(2,1)S(1)}, bf16[144,128]{1,0:T(8,128)(2,1)S(1)}, u32[]{:S(2)}, u32[]{:S(2)}) collective-permute-start(bf16[144,128]{1,0:T(8,128)(2,1)S(1)} %weigh.1.refs_0_), channel_id=1, source_target_pairs={{0,3},{1,2},{2,1},{3,0},{4,7},{5,6},{6,5},{7,4},{8,11},{9,10},{10,... | collective-permute-start | bytes 110600 | tf_op jit(solution)/shard_map/ppermute | solution.py:20
  34.4 1.2 %collective-permute-done.11.refs_2_ = bf16[144,128]{1,0:T(8,128)(2,1)S(1)} collective-permute-done((bf16[144,128]{1,0:T(8,128)(2,1)S(1)}, bf16[144,128]{1,0:T(8,128)(2,1)S(1)}, u32[]{:S(2)}, u32[]{:S(2)}) %collective-permute-start.11) | collective-permute-done | bytes 36896 | tf_op jit(solution)/shard_map/ppermute | solution.py:20
  35.6 2.6 %collective-permute-done.12.refs_3_ = bf16[144,128]{1,0:T(8,128)(2,1)S(1)} collective-permute-done((bf16[144,128]{1,0:T(8,128)(2,1)S(1)}, bf16[144,128]{1,0:T(8,128)(2,1)S(1)}, u32[]{:S(2)}, u32[]{:S(2)}) %collective-permute-start.12) | collective-permute-done | bytes 36896 | tf_op jit(solution)/shard_map/ppermute | solution.py:20
  38.1 0.7 %field.1 = (f32[64,4096]{1,0:T(8,128)S(1)}, bf16[32,4096]{1,0:T(8,128)(2,1)S(1)}, bf16[32,4096]{1,0:T(8,128)(2,1)S(1)}, f32[4,128]{1,0:T(4,128)S(1)}) custom-call(bf16[144,128]{1,0:T(8,128)(2,1)S(1)} %weigh.1.refs_0_, bf16[144,128]{1,0:T(8,128)(2,1)S(1)} %collective-permute-done.10.refs_1_, bf16[144,128]{1,0:T(8,128)(2,1)S(1)} %collective-permute-done.11.refs_2_, ...), custom_call_target="tpu_custom_call" | custom-call | flops 536870912 | bytes 4194304 | tf_op jit(solution)/shard_map/field/pallas_call | solution.py:243
  39.5 1.0 %collective-permute-done.14.got = bf16[32,4096]{1,0:T(8,128)(2,1)S(1)} collective-permute-done((bf16[32,4096]{1,0:T(8,128)(2,1)S(1)}, bf16[32,4096]{1,0:T(8,128)(2,1)S(1)}, u32[]{:S(2)}, u32[]{:S(2)}) %collective-permute-start.14) | collective-permute-done | bytes 262176 | tf_op jit(solution)/shard_map/ppermute | solution.py:20
  40.5 1.3 %collective-permute-start.15 = (bf16[16,4096]{1,0:T(8,128)(2,1)S(1)}, bf16[16,4096]{1,0:T(8,128)(2,1)S(1)}, u32[]{:S(2)}, u32[]{:S(2)}) collective-permute-start(bf16[16,4096]{1,0:T(8,128)(2,1)S(1)} %get-tuple-element.32), channel_id=1, source_target_pairs={{0,8},{4,12},{8,0},{12,4},{16,24},{20,28},{24,16},{28,20},{1,9},{5... | collective-permute-start | bytes 393224 | tf_op jit(solution)/shard_map/ppermute | solution.py:20
  41.8 0.8 %collective-permute-start.16 = (bf16[16,4096]{1,0:T(8,128)(2,1)S(1)}, bf16[16,4096]{1,0:T(8,128)(2,1)S(1)}, u32[]{:S(2)}, u32[]{:S(2)}) collective-permute-start(bf16[16,4096]{1,0:T(8,128)(2,1)S(1)} %get-tuple-element.33), channel_id=1, source_target_pairs={{0,16},{4,20},{8,24},{12,28},{16,0},{20,4},{24,8},{28,12},{1,17},{... | collective-permute-start | bytes 393224 | tf_op jit(solution)/shard_map/ppermute | solution.py:20
  42.7 1.5 %collective-permute-start.17 = (bf16[16,4096]{1,0:T(8,128)(2,1)S(1)}, bf16[16,4096]{1,0:T(8,128)(2,1)S(1)}, u32[]{:S(2)}, u32[]{:S(2)}) collective-permute-start(bf16[16,4096]{1,0:T(8,128)(2,1)S(1)} %get-tuple-element.34), channel_id=1, source_target_pairs={{0,24},{4,28},{8,16},{12,20},{16,8},{20,12},{24,0},{28,4},{1,25},{... | collective-permute-start | bytes 393224 | tf_op jit(solution)/shard_map/ppermute | solution.py:20
  44.8 1.9 %collective-permute-done.15.refs_0_ = bf16[16,4096]{1,0:T(8,128)(2,1)S(1)} collective-permute-done((bf16[16,4096]{1,0:T(8,128)(2,1)S(1)}, bf16[16,4096]{1,0:T(8,128)(2,1)S(1)}, u32[]{:S(2)}, u32[]{:S(2)}) %collective-permute-start.15) | collective-permute-done | bytes 131104 | tf_op jit(solution)/shard_map/ppermute | solution.py:20
  46.7 1.6 %collective-permute-done.16.refs_1_ = bf16[16,4096]{1,0:T(8,128)(2,1)S(1)} collective-permute-done((bf16[16,4096]{1,0:T(8,128)(2,1)S(1)}, bf16[16,4096]{1,0:T(8,128)(2,1)S(1)}, u32[]{:S(2)}, u32[]{:S(2)}) %collective-permute-start.16) | collective-permute-done | bytes 131104 | tf_op jit(solution)/shard_map/ppermute | solution.py:20
  48.3 1.6 %collective-permute-done.17.refs_2_ = bf16[16,4096]{1,0:T(8,128)(2,1)S(1)} collective-permute-done((bf16[16,4096]{1,0:T(8,128)(2,1)S(1)}, bf16[16,4096]{1,0:T(8,128)(2,1)S(1)}, u32[]{:S(2)}, u32[]{:S(2)}) %collective-permute-start.17) | collective-permute-done | bytes 131104 | tf_op jit(solution)/shard_map/ppermute | solution.py:20
  49.9 0.8 %final.1 = f32[16,4096]{1,0:T(8,128)} custom-call(f32[16,4096]{1,0:T(8,128)S(1)} %get-tuple-element.30.own, bf16[16,4096]{1,0:T(8,128)(2,1)S(1)} %collective-permute-done.15.refs_0_, bf16[16,4096]{1,0:T(8,128)(2,1)S(1)} %collective-permute-done.16.refs_1_, bf16[16,4096]{1,0:T(8,128)(2,1)S(1)} %collective-permute-done.17.refs_2_), custom_call_target="tpu_custom_call" | custom-call | flops 196608 | bytes 786432 | tf_op jit(solution)/shard_map/final/pallas_call | solution.py:289
  (23 shorter events, 2.3 us)
Async XLA Ops:
  0.6 7.2 %collective-permute-start = (bf16[16,4096]{1,0:T(8,128)(2,1)}, bf16[16,4096]{1,0:T(8,128)(2,1)S(1)}, u32[]{:S(2)}, u32[]{:S(2)}) collective-permute-start(bf16[16,4096]{1,0:T(8,128)(2,1)} %refs_2_.1), channel_id=1, source_target_pairs={{0,8},{4,12},{8,0},{12,4},{16,24},{20,28},{24,16},{28,20},{1,9},{5... | collective-permute-start | bytes 393224 | tf_op jit(solution)/shard_map/ppermute | solution.py:20
  3.7 8.0 %collective-permute-start.2 = (bf16[16,4096]{1,0:T(8,128)(2,1)}, bf16[16,4096]{1,0:T(8,128)(2,1)S(1)}, u32[]{:S(2)}, u32[]{:S(2)}) collective-permute-start(bf16[16,4096]{1,0:T(8,128)(2,1)} %refs_2_.1), channel_id=1, source_target_pairs={{0,16},{4,20},{8,24},{12,28},{16,0},{20,4},{24,8},{28,12},{1,17},{... | collective-permute-start | bytes 393224 | tf_op jit(solution)/shard_map/ppermute | solution.py:20
  5.2 6.5 %collective-permute-start.5 = (bf16[16,4096]{1,0:T(8,128)(2,1)}, bf16[16,4096]{1,0:T(8,128)(2,1)S(1)}, u32[]{:S(2)}, u32[]{:S(2)}) collective-permute-start(bf16[16,4096]{1,0:T(8,128)(2,1)} %refs_2_.1), channel_id=1, source_target_pairs={{0,24},{4,28},{8,16},{12,20},{16,8},{20,12},{24,0},{28,4},{1,25},{... | collective-permute-start | bytes 393224 | tf_op jit(solution)/shard_map/ppermute | solution.py:20
  5.2 11.7 %collective-permute-start.4 = (bf16[16,4096]{1,0:T(8,128)(2,1)}, bf16[16,4096]{1,0:T(8,128)(2,1)S(1)}, u32[]{:S(2)}, u32[]{:S(2)}) collective-permute-start(bf16[16,4096]{1,0:T(8,128)(2,1)} %refs_2_.1), channel_id=1, source_target_pairs={{0,4},{4,0},{8,12},{12,8},{16,20},{20,16},{24,28},{28,24},{1,5},{5... | collective-permute-start | bytes 393224 | tf_op jit(solution)/shard_map/ppermute | solution.py:20
  7.9 9.1 %collective-permute-start.1 = (bf16[16,4096]{1,0:T(8,128)(2,1)S(1)}, bf16[16,4096]{1,0:T(8,128)(2,1)S(1)}, u32[]{:S(2)}, u32[]{:S(2)}) collective-permute-start(bf16[16,4096]{1,0:T(8,128)(2,1)S(1)} %collective-permute-done.refs_0_), channel_id=1, source_target_pairs={{0,4},{4,0},{8,12},{12,8},{16,20},{20,16},{24,28},{28,24},{1,5},{5... | collective-permute-start | bytes 393224 | tf_op jit(solution)/shard_map/ppermute | solution.py:20
  11.7 5.3 %collective-permute-start.3 = (bf16[16,4096]{1,0:T(8,128)(2,1)S(1)}, bf16[16,4096]{1,0:T(8,128)(2,1)S(1)}, u32[]{:S(2)}, u32[]{:S(2)}) collective-permute-start(bf16[16,4096]{1,0:T(8,128)(2,1)S(1)} %collective-permute-done.2.refs_1_), channel_id=1, source_target_pairs={{0,4},{4,0},{8,12},{12,8},{16,20},{20,16},{24,28},{28,24},{1,5},{5... | collective-permute-start | bytes 393224 | tf_op jit(solution)/shard_map/ppermute | solution.py:20
  11.7 5.3 %collective-permute-start.6 = (bf16[16,4096]{1,0:T(8,128)(2,1)S(1)}, bf16[16,4096]{1,0:T(8,128)(2,1)S(1)}, u32[]{:S(2)}, u32[]{:S(2)}) collective-permute-start(bf16[16,4096]{1,0:T(8,128)(2,1)S(1)} %collective-permute-done.5.refs_3_), channel_id=1, source_target_pairs={{0,4},{4,0},{8,12},{12,8},{16,20},{20,16},{24,28},{28,24},{1,5},{5... | collective-permute-start | bytes 393224 | tf_op jit(solution)/shard_map/ppermute | solution.py:20
  12.2 4.6 %copy-start = (bf16[16,4096]{1,0:T(8,128)(2,1)S(1)}, bf16[16,4096]{1,0:T(8,128)(2,1)}, u32[]{:S(2)}) copy-start(bf16[16,4096]{1,0:T(8,128)(2,1)} %refs_2_.1) | copy-start | bytes 393220
  19.4 5.1 %collective-permute-start.7 = (f32[128,128]{1,0:T(8,128)S(1)}, f32[128,128]{1,0:T(8,128)S(1)}, u32[]{:S(2)}, u32[]{:S(2)}) collective-permute-start(f32[128,128]{1,0:T(8,128)S(1)} %get-tuple-element.24), channel_id=1, source_target_pairs={{0,1},{1,0},{2,3},{3,2},{4,5},{5,4},{6,7},{7,6},{8,9},{9,8},{10,11... | collective-permute-start | bytes 196616 | tf_op jit(solution)/shard_map/ppermute | solution.py:20
  21.1 7.5 %collective-permute-start.8 = (f32[128,128]{1,0:T(8,128)S(1)}, f32[128,128]{1,0:T(8,128)S(1)}, u32[]{:S(2)}, u32[]{:S(2)}) collective-permute-start(f32[128,128]{1,0:T(8,128)S(1)} %get-tuple-element.25), channel_id=1, source_target_pairs={{0,2},{1,3},{2,0},{3,1},{4,6},{5,7},{6,4},{7,5},{8,10},{9,11},{10,... | collective-permute-start | bytes 196616 | tf_op jit(solution)/shard_map/ppermute | solution.py:20
  23.7 6.2 %collective-permute-start.9 = (f32[128,128]{1,0:T(8,128)S(1)}, f32[128,128]{1,0:T(8,128)S(1)}, u32[]{:S(2)}, u32[]{:S(2)}) collective-permute-start(f32[128,128]{1,0:T(8,128)S(1)} %get-tuple-element.26), channel_id=1, source_target_pairs={{0,3},{1,2},{2,1},{3,0},{4,7},{5,6},{6,5},{7,4},{8,11},{9,10},{10,... | collective-permute-start | bytes 196616 | tf_op jit(solution)/shard_map/ppermute | solution.py:20
  29.9 4.5 %collective-permute-start.10 = (bf16[144,128]{1,0:T(8,128)(2,1)S(1)}, bf16[144,128]{1,0:T(8,128)(2,1)S(1)}, u32[]{:S(2)}, u32[]{:S(2)}) collective-permute-start(bf16[144,128]{1,0:T(8,128)(2,1)S(1)} %weigh.1.refs_0_), channel_id=1, source_target_pairs={{0,1},{1,0},{2,3},{3,2},{4,5},{5,4},{6,7},{7,6},{8,9},{9,8},{10,11... | collective-permute-start | bytes 110600 | tf_op jit(solution)/shard_map/ppermute | solution.py:20
  30.7 4.9 %collective-permute-start.11 = (bf16[144,128]{1,0:T(8,128)(2,1)S(1)}, bf16[144,128]{1,0:T(8,128)(2,1)S(1)}, u32[]{:S(2)}, u32[]{:S(2)}) collective-permute-start(bf16[144,128]{1,0:T(8,128)(2,1)S(1)} %weigh.1.refs_0_), channel_id=1, source_target_pairs={{0,2},{1,3},{2,0},{3,1},{4,6},{5,7},{6,4},{7,5},{8,10},{9,11},{10,... | collective-permute-start | bytes 110600 | tf_op jit(solution)/shard_map/ppermute | solution.py:20
  32.4 5.8 %collective-permute-start.12 = (bf16[144,128]{1,0:T(8,128)(2,1)S(1)}, bf16[144,128]{1,0:T(8,128)(2,1)S(1)}, u32[]{:S(2)}, u32[]{:S(2)}) collective-permute-start(bf16[144,128]{1,0:T(8,128)(2,1)S(1)} %weigh.1.refs_0_), channel_id=1, source_target_pairs={{0,3},{1,2},{2,1},{3,0},{4,7},{5,6},{6,5},{7,4},{8,11},{9,10},{10,... | collective-permute-start | bytes 110600 | tf_op jit(solution)/shard_map/ppermute | solution.py:20
  38.9 1.6 %collective-permute-start.14 = (bf16[32,4096]{1,0:T(8,128)(2,1)S(1)}, bf16[32,4096]{1,0:T(8,128)(2,1)S(1)}, u32[]{:S(2)}, u32[]{:S(2)}) collective-permute-start(bf16[32,4096]{1,0:T(8,128)(2,1)S(1)} %get-tuple-element.31), channel_id=1, source_target_pairs={{0,4},{4,0},{8,12},{12,8},{16,20},{20,16},{24,28},{28,24},{1,5},{5... | collective-permute-start | bytes 786440 | tf_op jit(solution)/shard_map/ppermute | solution.py:20
  39.0 3.7 %collective-permute-start.13 = (bf16[32,4096]{1,0:T(8,128)(2,1)S(1)}, bf16[32,4096]{1,0:T(8,128)(2,1)S(1)}, u32[]{:S(2)}, u32[]{:S(2)}) collective-permute-start(bf16[32,4096]{1,0:T(8,128)(2,1)S(1)} %get-tuple-element.29), channel_id=1, source_target_pairs={{0,4},{4,0},{8,12},{12,8},{16,20},{20,16},{24,28},{28,24},{1,5},{5... | collective-permute-start | bytes 786440 | tf_op jit(solution)/shard_map/ppermute | solution.py:20
  40.5 6.2 %collective-permute-start.15 = (bf16[16,4096]{1,0:T(8,128)(2,1)S(1)}, bf16[16,4096]{1,0:T(8,128)(2,1)S(1)}, u32[]{:S(2)}, u32[]{:S(2)}) collective-permute-start(bf16[16,4096]{1,0:T(8,128)(2,1)S(1)} %get-tuple-element.32), channel_id=1, source_target_pairs={{0,8},{4,12},{8,0},{12,4},{16,24},{20,28},{24,16},{28,20},{1,9},{5... | collective-permute-start | bytes 393224 | tf_op jit(solution)/shard_map/ppermute | solution.py:20
  41.8 6.4 %collective-permute-start.16 = (bf16[16,4096]{1,0:T(8,128)(2,1)S(1)}, bf16[16,4096]{1,0:T(8,128)(2,1)S(1)}, u32[]{:S(2)}, u32[]{:S(2)}) collective-permute-start(bf16[16,4096]{1,0:T(8,128)(2,1)S(1)} %get-tuple-element.33), channel_id=1, source_target_pairs={{0,16},{4,20},{8,24},{12,28},{16,0},{20,4},{24,8},{28,12},{1,17},{... | collective-permute-start | bytes 393224 | tf_op jit(solution)/shard_map/ppermute | solution.py:20
  42.7 7.2 %collective-permute-start.17 = (bf16[16,4096]{1,0:T(8,128)(2,1)S(1)}, bf16[16,4096]{1,0:T(8,128)(2,1)S(1)}, u32[]{:S(2)}, u32[]{:S(2)}) collective-permute-start(bf16[16,4096]{1,0:T(8,128)(2,1)S(1)} %get-tuple-element.34), channel_id=1, source_target_pairs={{0,24},{4,28},{8,16},{12,20},{16,8},{20,12},{24,0},{28,4},{1,25},{... | collective-permute-start | bytes 393224 | tf_op jit(solution)/shard_map/ppermute | solution.py:20

commit v2 on v1

--- a/solution.py
+++ b/solution.py
@@ -37,8 +37,11 @@
         small.append(pltpu.make_async_copy(source, target, small_sem.at[i]))
         small[-1].start()
     loads = []
+    quarter = lax.axis_index("pix")
+    lanes = prior.shape[1]
     for s in range(steps):
-        span = pl.ds(s * tall, tall)
+        first = (quarter ^ (s * tall // lanes)) * lanes + s * tall % lanes
+        span = pl.ds(pl.multiple_of(first, tall), tall)
         a = pltpu.make_async_copy(particles.at[span], p_buf.at[s], p_sem.at[s])
         b = pltpu.make_async_copy(ctf.at[span], c_buf.at[s], c_sem.at[s])
         loads.append((a, b))
@@ -76,7 +79,7 @@
 
 def prepare(order, rows, parts, particles, ctf, noise, orient_class, class_prior):
     slots, pixels = particles.shape
-    steps = 8 if slots % 128 == 0 else 1
+    steps = 2 * parts
     orients = orient_class.shape[1]
     operands = (particles, ctf, noise, orient_class, class_prior)
     return pl.pallas_call(
@@ -131,11 +134,10 @@
 NT = (((1,), (1,)), ((), ()))
 
 
-def score_kernel(pieces, parts, *refs):
+def score_kernel(pieces, *refs):
     proj = refs[:pieces]
     lines, square, weighted, quadratic = refs[pieces : pieces + 4]
-    outs = refs[pieces + 4 : pieces + 4 + parts]
-    lines_all, square_all, total = refs[pieces + 4 + parts :]
+    *outs, lines_all, square_all = refs[pieces + 4 :]
     rows = proj[0].shape[0]
     first = lines.shape[0]
     lines_all[:first, :] = lines[...]
@@ -146,14 +148,12 @@
         span = slice(first + i * rows, first + (i + 1) * rows)
         lines_all[span, :] = value
         square_all[span, :] = (-0.5 * wide * wide).astype(BF16)
-    total[...] = lax.dot_general(weighted[...], lines_all[...], NT, preferred_element_type=F32) + lax.dot_general(
-        quadratic[...], square_all[...], NT, preferred_element_type=F32
+    lanes = outs[0].shape[1]
+    total = lax.dot_general(weighted[lanes:, :], lines_all[...], NT, preferred_element_type=F32) + lax.dot_general(
+        quadratic[lanes:, :], square_all[...], NT, preferred_element_type=F32
     )
-    quarter = lax.axis_index("pix")
-    lanes = outs[0].shape[1]
     for j, out in enumerate(outs):
-        start = pl.multiple_of((quarter ^ j) * lanes, lanes)
-        out[...] = total[pl.ds(start, lanes), :].T
+        out[...] = total[j * lanes : (j + 1) * lanes, :].T
 
 
 def score(parts, proj, lines, square, weighted, quadratic):
@@ -161,19 +161,37 @@
     orients = rows * len(proj) + lines.shape[0]
     slots = weighted.shape[0]
     return pl.pallas_call(
-        functools.partial(score_kernel, len(proj), parts),
-        out_shape=tuple(pltpu.VMEM((orients, slots // parts), F32) for _ in range(parts)),
+        functools.partial(score_kernel, len(proj)),
+        out_shape=tuple(pltpu.VMEM((orients, slots // parts), F32) for _ in range(parts - 1))
+        + (pltpu.VMEM((orients, pixels), BF16),) * 2,
         in_specs=[VMEM] * (len(proj) + 4),
-        out_specs=(VMEM,) * parts,
-        scratch_shapes=[
-            pltpu.VMEM((orients, pixels), BF16),
-            pltpu.VMEM((orients, pixels), BF16),
-            pltpu.VMEM((slots, orients), F32),
-        ],
-        compiler_params=params(28),
+        out_specs=(VMEM,) * (parts + 1),
+        compiler_params=params(12),
         cost_estimate=cost(4 * orients * slots * pixels, 4 * slots * pixels),
         name="score",
     )(*proj, lines, square, weighted, quadratic)
+
+
+def own_kernel(lines, square, weighted, quadratic, out):
+    lanes = out.shape[1]
+    total = lax.dot_general(weighted[:lanes, :], lines[...], NT, preferred_element_type=F32) + lax.dot_general(
+        quadratic[:lanes, :], square[...], NT, preferred_element_type=F32
+    )
+    out[...] = total.T
+
+
+def own_score(parts, lines, square, weighted, quadratic):
+    orients, pixels = lines.shape
+    lanes = weighted.shape[0] // parts
+    return pl.pallas_call(
+        own_kernel,
+        out_shape=pltpu.VMEM((orients, lanes), F32),
+        in_specs=[VMEM] * 4,
+        out_specs=VMEM,
+        compiler_params=params(12),
+        cost_estimate=cost(4 * orients * lanes * pixels, 4 * lanes * pixels),
+        name="own_score",
+    )(lines, square, weighted, quadratic)
 
 
 def weigh_kernel(parts, *refs):
@@ -220,8 +238,7 @@
     quarter = lax.axis_index("pix")
     for j, piece in enumerate(pieces):
         place = quarter ^ j
-        start = pl.multiple_of(place * lanes, lanes)
-        lhs[:, pl.ds(start, lanes)] = piece[:orients, :]
+        lhs[:, j * lanes : (j + 1) * lanes] = piece[:orients, :]
         tail = piece[orients:, :].astype(F32)
         norm[pl.ds(place, 1), :] = (tail[0:1] + tail[1:2]) + tail[2:3]
     half = orients // 2
@@ -312,10 +329,11 @@
     for k in even:
         near[k] = swap(far[k], "blk", blk, 1)
     lines, square = squares([far[k] for k in lead])
-    chunks = score(pix, [near[k] for k in lead], lines, square, weighted, quadratic)
-    pieces = [chunks[0]]
+    *chunks, lines, square = score(pix, [near[k] for k in lead], lines, square, weighted, quadratic)
+    pieces = []
     for j in range(1, pix):
-        pieces.append(swap(chunks[j], "pix", pix, j))
+        pieces.append(swap(chunks[j - 1], "pix", pix, j))
+    pieces.insert(0, own_score(pix, lines, square, weighted, quadratic))
     weights = weigh(pieces, prior, counts)
     parts = [weights]
     for j in range(1, pix):

time: 50.8 us -> 50.2 us (0.988)
  waiting for transfers between devices: 21.7 us -> 20.9 us
    ppermute x18, waiting for transfers between devices: 21.7 us -> 20.9 us  [swap(): out = lax.ppermute(value, axis, [(i, i ^ k) for i in range(size)])]
    pallas_call x1 -> x2, Pallas kernels: 2.46 us -> 2.63 us  [the longest x1 1.86 us: score(): pl.pallas_call(functools.partial(score_kernel, len(proj)), out_shape=tupl...]
  transfers between devices with their start and end apart: 18 -> 18, of which waited for: 10 -> 10; matrix products, arithmetic and copies ran while one was open for 1% -> 1% of each run, Pallas kernels for 10% -> 11%
where the time goes in v2:
time: 50.2 us; the launch traced here: 50.1 us
  waiting for transfers between devices  20.9 us (42%)
  starting transfers between devices  18.2 us (36%)
  Pallas kernels  9.01 us (18%)
  between operations  1.4 us (3%)
  local copies, waits for them, and re-layouts  0.58 us (1%)
    ppermute x18, waiting for transfers between devices, swap(): out = lax.ppermute(value, axis, [(i, i ^ k) for i in range(size)])  20.9 us
    ppermute x18, starting transfers between devices, swap(): out = lax.ppermute(value, axis, [(i, i ^ k) for i in range(size)])  18.2 us
    pallas_call x1, Pallas kernels, prepare(): pl.pallas_call(functools.partial(prepare_kernel, order, rows), out_shape=...  4.55 us
    pallas_call x1, Pallas kernels, score(): pl.pallas_call(functools.partial(score_kernel, len(proj)), out_shape=tupl...  1.86 us
  transfers between devices with their start and end apart: 18, of which 10 were waited for; matrix products, arithmetic and copies ran while one was open for 1% of the time, Pallas kernels for 11%

profile of v2, /device:TPU:0, one launch (start us, length us, event | category | flops | bytes accessed | tf_op | source)
XLA Modules:
  0.0 50.1 jit_solution(14251687871105825663)
XLA Ops:
  0.6 3.0 %collective-permute-start = (bf16[16,4096]{1,0:T(8,128)(2,1)}, bf16[16,4096]{1,0:T(8,128)(2,1)S(1)}, u32[]{:S(2)}, u32[]{:S(2)}) collective-permute-start(bf16[16,4096]{1,0:T(8,128)(2,1)} %refs_2_.1), channel_id=1, source_target_pairs={{0,8},{4,12},{8,0},{12,4},{16,24},{20,28},{24,16},{28,20},{1,9},{5... | collective-permute-start | bytes 393224 | tf_op jit(solution)/shard_map/ppermute | solution.py:20
  3.7 1.5 %collective-permute-start.2 = (bf16[16,4096]{1,0:T(8,128)(2,1)}, bf16[16,4096]{1,0:T(8,128)(2,1)S(1)}, u32[]{:S(2)}, u32[]{:S(2)}) collective-permute-start(bf16[16,4096]{1,0:T(8,128)(2,1)} %refs_2_.1), channel_id=1, source_target_pairs={{0,16},{4,20},{8,24},{12,28},{16,0},{20,4},{24,8},{28,12},{1,17},{... | collective-permute-start | bytes 393224 | tf_op jit(solution)/shard_map/ppermute | solution.py:20
  5.2 2.7 %collective-permute-done.refs_0_ = bf16[16,4096]{1,0:T(8,128)(2,1)S(1)} collective-permute-done((bf16[16,4096]{1,0:T(8,128)(2,1)}, bf16[16,4096]{1,0:T(8,128)(2,1)S(1)}, u32[]{:S(2)}, u32[]{:S(2)}) %collective-permute-start) | collective-permute-done | bytes 131104 | tf_op jit(solution)/shard_map/ppermute | solution.py:20
  7.9 3.8 %collective-permute-done.2.refs_1_ = bf16[16,4096]{1,0:T(8,128)(2,1)S(1)} collective-permute-done((bf16[16,4096]{1,0:T(8,128)(2,1)}, bf16[16,4096]{1,0:T(8,128)(2,1)S(1)}, u32[]{:S(2)}, u32[]{:S(2)}) %collective-permute-start.2) | collective-permute-done | bytes 131104 | tf_op jit(solution)/shard_map/ppermute | solution.py:20
  12.2 4.5 %prepare.1 = (bf16[512,4096]{1,0:T(8,128)(2,1)S(1)}, bf16[512,4096]{1,0:T(8,128)(2,1)S(1)}, f32[128,128]{1,0:T(8,128)S(1)}) custom-call(bf16[512,4096]{1,0:T(8,128)(2,1)} %particles.1, bf16[512,4096]{1,0:T(8,128)(2,1)} %ctf.1, f32[1,4096]{1,0:T(1,128)} %bitcast.5, s32[1,128]{1,0:T(1,128)} %bitcast.6, f32[1,5]{1,0:T(1,128)} %bitcast.7), custom_call_target="tpu_custom_call" | custom-call | flops 33554432 | bytes 16777216 | tf_op jit(solution)/shard_map/prepare/pallas_call | solution.py:85
  16.9 1.9 %score.1 = (f32[128,128]{1,0:T(8,128)S(1)}, f32[128,128]{1,0:T(8,128)S(1)}, f32[128,128]{1,0:T(8,128)S(1)}, bf16[128,4096]{1,0:T(8,128)(2,1)S(1)}, bf16[128,4096]{1,0:T(8,128)(2,1)S(1)}) custom-call(bf16[16,4096]{1,0:T(8,128)(2,1)S(1)} %collective-permute-done.1.refs_0_, bf16[16,4096]{1,0:T(8,128)(2,1)S(1)} %collective-permute-done.3.refs_1_, ...), custom_call_target="tpu_custom_call" | custom-call | flops 1073741824 | bytes 8388608 | tf_op jit(solution)/shard_map/score/pallas_call | solution.py:163
  18.8 1.6 %collective-permute-start.7 = (f32[128,128]{1,0:T(8,128)S(1)}, f32[128,128]{1,0:T(8,128)S(1)}, u32[]{:S(2)}, u32[]{:S(2)}) collective-permute-start(f32[128,128]{1,0:T(8,128)S(1)} %get-tuple-element.26), channel_id=1, source_target_pairs={{0,1},{1,0},{2,3},{3,2},{4,5},{5,4},{6,7},{7,6},{8,9},{9,8},{10,11... | collective-permute-start | bytes 196616 | tf_op jit(solution)/shard_map/ppermute | solution.py:20
  20.5 2.6 %collective-permute-start.8 = (f32[128,128]{1,0:T(8,128)S(1)}, f32[128,128]{1,0:T(8,128)S(1)}, u32[]{:S(2)}, u32[]{:S(2)}) collective-permute-start(f32[128,128]{1,0:T(8,128)S(1)} %get-tuple-element.27), channel_id=1, source_target_pairs={{0,2},{1,3},{2,0},{3,1},{4,6},{5,7},{6,4},{7,5},{8,10},{9,11},{10,... | collective-permute-start | bytes 196616 | tf_op jit(solution)/shard_map/ppermute | solution.py:20
  23.9 0.8 %own_score.1.refs_0_ = f32[128,128]{1,0:T(8,128)S(1)} custom-call(bf16[128,4096]{1,0:T(8,128)(2,1)S(1)} %get-tuple-element.24.lines, bf16[128,4096]{1,0:T(8,128)(2,1)S(1)} %get-tuple-element.25.square, bf16[512,4096]{1,0:T(8,128)(2,1)S(1)} %get-tuple-element.22.refs_6_.weighted.refs_4_, bf16[512,4096]{1,0:T(8,128)(2,1)S(1)} %get-tuple-element.23.refs_7_.quadratic), custom_call_target="tpu_custom_call" | custom-call | flops 268435456 | bytes 2097152 | tf_op jit(solution)/shard_map/own_score/pallas_call | solution.py:186
  24.7 3.2 %collective-permute-done.8.refs_2_ = f32[128,128]{1,0:T(8,128)S(1)} collective-permute-done((f32[128,128]{1,0:T(8,128)S(1)}, f32[128,128]{1,0:T(8,128)S(1)}, u32[]{:S(2)}, u32[]{:S(2)}) %collective-permute-start.8) | collective-permute-done | bytes 65568 | tf_op jit(solution)/shard_map/ppermute | solution.py:20
  27.9 1.3 %collective-permute-done.9.refs_3_ = f32[128,128]{1,0:T(8,128)S(1)} collective-permute-done((f32[128,128]{1,0:T(8,128)S(1)}, f32[128,128]{1,0:T(8,128)S(1)}, u32[]{:S(2)}, u32[]{:S(2)}) %collective-permute-start.9) | collective-permute-done | bytes 65568 | tf_op jit(solution)/shard_map/ppermute | solution.py:20
  29.3 0.8 %collective-permute-start.10 = (bf16[144,128]{1,0:T(8,128)(2,1)S(1)}, bf16[144,128]{1,0:T(8,128)(2,1)S(1)}, u32[]{:S(2)}, u32[]{:S(2)}) collective-permute-start(bf16[144,128]{1,0:T(8,128)(2,1)S(1)} %weigh.1.refs_0_), channel_id=1, source_target_pairs={{0,1},{1,0},{2,3},{3,2},{4,5},{5,4},{6,7},{7,6},{8,9},{9,8},{10,11... | collective-permute-start | bytes 110600 | tf_op jit(solution)/shard_map/ppermute | solution.py:20
  30.1 1.7 %collective-permute-start.11 = (bf16[144,128]{1,0:T(8,128)(2,1)S(1)}, bf16[144,128]{1,0:T(8,128)(2,1)S(1)}, u32[]{:S(2)}, u32[]{:S(2)}) collective-permute-start(bf16[144,128]{1,0:T(8,128)(2,1)S(1)} %weigh.1.refs_0_), channel_id=1, source_target_pairs={{0,2},{1,3},{2,0},{3,1},{4,6},{5,7},{6,4},{7,5},{8,10},{9,11},{10,... | collective-permute-start | bytes 110600 | tf_op jit(solution)/shard_map/ppermute | solution.py:20
  31.8 2.0 %collective-permute-start.12 = (bf16[144,128]{1,0:T(8,128)(2,1)S(1)}, bf16[144,128]{1,0:T(8,128)(2,1)S(1)}, u32[]{:S(2)}, u32[]{:S(2)}) collective-permute-start(bf16[144,128]{1,0:T(8,128)(2,1)S(1)} %weigh.1.refs_0_), channel_id=1, source_target_pairs={{0,3},{1,2},{2,1},{3,0},{4,7},{5,6},{6,5},{7,4},{8,11},{9,10},{10,... | collective-permute-start | bytes 110600 | tf_op jit(solution)/shard_map/ppermute | solution.py:20
  33.8 1.2 %collective-permute-done.11.refs_2_ = bf16[144,128]{1,0:T(8,128)(2,1)S(1)} collective-permute-done((bf16[144,128]{1,0:T(8,128)(2,1)S(1)}, bf16[144,128]{1,0:T(8,128)(2,1)S(1)}, u32[]{:S(2)}, u32[]{:S(2)}) %collective-permute-start.11) | collective-permute-done | bytes 36896 | tf_op jit(solution)/shard_map/ppermute | solution.py:20
  35.0 2.6 %collective-permute-done.12.refs_3_ = bf16[144,128]{1,0:T(8,128)(2,1)S(1)} collective-permute-done((bf16[144,128]{1,0:T(8,128)(2,1)S(1)}, bf16[144,128]{1,0:T(8,128)(2,1)S(1)}, u32[]{:S(2)}, u32[]{:S(2)}) %collective-permute-start.12) | collective-permute-done | bytes 36896 | tf_op jit(solution)/shard_map/ppermute | solution.py:20
  38.9 1.0 %collective-permute-done.14.got = bf16[32,4096]{1,0:T(8,128)(2,1)S(1)} collective-permute-done((bf16[32,4096]{1,0:T(8,128)(2,1)S(1)}, bf16[32,4096]{1,0:T(8,128)(2,1)S(1)}, u32[]{:S(2)}, u32[]{:S(2)}) %collective-permute-start.14) | collective-permute-done | bytes 262176 | tf_op jit(solution)/shard_map/ppermute | solution.py:20
  39.9 1.3 %collective-permute-start.15 = (bf16[16,4096]{1,0:T(8,128)(2,1)S(1)}, bf16[16,4096]{1,0:T(8,128)(2,1)S(1)}, u32[]{:S(2)}, u32[]{:S(2)}) collective-permute-start(bf16[16,4096]{1,0:T(8,128)(2,1)S(1)} %get-tuple-element.34), channel_id=1, source_target_pairs={{0,8},{4,12},{8,0},{12,4},{16,24},{20,28},{24,16},{28,20},{1,9},{5... | collective-permute-start | bytes 393224 | tf_op jit(solution)/shard_map/ppermute | solution.py:20
  41.2 0.8 %collective-permute-start.16 = (bf16[16,4096]{1,0:T(8,128)(2,1)S(1)}, bf16[16,4096]{1,0:T(8,128)(2,1)S(1)}, u32[]{:S(2)}, u32[]{:S(2)}) collective-permute-start(bf16[16,4096]{1,0:T(8,128)(2,1)S(1)} %get-tuple-element.35), channel_id=1, source_target_pairs={{0,16},{4,20},{8,24},{12,28},{16,0},{20,4},{24,8},{28,12},{1,17},{... | collective-permute-start | bytes 393224 | tf_op jit(solution)/shard_map/ppermute | solution.py:20
  42.1 1.5 %collective-permute-start.17 = (bf16[16,4096]{1,0:T(8,128)(2,1)S(1)}, bf16[16,4096]{1,0:T(8,128)(2,1)S(1)}, u32[]{:S(2)}, u32[]{:S(2)}) collective-permute-start(bf16[16,4096]{1,0:T(8,128)(2,1)S(1)} %get-tuple-element.36), channel_id=1, source_target_pairs={{0,24},{4,28},{8,16},{12,20},{16,8},{20,12},{24,0},{28,4},{1,25},{... | collective-permute-start | bytes 393224 | tf_op jit(solution)/shard_map/ppermute | solution.py:20
  44.2 1.9 %collective-permute-done.15.refs_0_ = bf16[16,4096]{1,0:T(8,128)(2,1)S(1)} collective-permute-done((bf16[16,4096]{1,0:T(8,128)(2,1)S(1)}, bf16[16,4096]{1,0:T(8,128)(2,1)S(1)}, u32[]{:S(2)}, u32[]{:S(2)}) %collective-permute-start.15) | collective-permute-done | bytes 131104 | tf_op jit(solution)/shard_map/ppermute | solution.py:20
  46.1 1.5 %collective-permute-done.16.refs_1_ = bf16[16,4096]{1,0:T(8,128)(2,1)S(1)} collective-permute-done((bf16[16,4096]{1,0:T(8,128)(2,1)S(1)}, bf16[16,4096]{1,0:T(8,128)(2,1)S(1)}, u32[]{:S(2)}, u32[]{:S(2)}) %collective-permute-start.16) | collective-permute-done | bytes 131104 | tf_op jit(solution)/shard_map/ppermute | solution.py:20
  47.7 1.6 %collective-permute-done.17.refs_2_ = bf16[16,4096]{1,0:T(8,128)(2,1)S(1)} collective-permute-done((bf16[16,4096]{1,0:T(8,128)(2,1)S(1)}, bf16[16,4096]{1,0:T(8,128)(2,1)S(1)}, u32[]{:S(2)}, u32[]{:S(2)}) %collective-permute-start.17) | collective-permute-done | bytes 131104 | tf_op jit(solution)/shard_map/ppermute | solution.py:20
  49.3 0.8 %final.1 = f32[16,4096]{1,0:T(8,128)} custom-call(f32[16,4096]{1,0:T(8,128)S(1)} %get-tuple-element.32.own, bf16[16,4096]{1,0:T(8,128)(2,1)S(1)} %collective-permute-done.15.refs_0_, bf16[16,4096]{1,0:T(8,128)(2,1)S(1)} %collective-permute-done.16.refs_1_, bf16[16,4096]{1,0:T(8,128)(2,1)S(1)} %collective-permute-done.17.refs_2_), custom_call_target="tpu_custom_call" | custom-call | flops 196608 | bytes 786432 | tf_op jit(solution)/shard_map/final/pallas_call | solution.py:306
  (24 shorter events, 3.0 us)
Async XLA Ops:
  0.6 7.2 %collective-permute-start = (bf16[16,4096]{1,0:T(8,128)(2,1)}, bf16[16,4096]{1,0:T(8,128)(2,1)S(1)}, u32[]{:S(2)}, u32[]{:S(2)}) collective-permute-start(bf16[16,4096]{1,0:T(8,128)(2,1)} %refs_2_.1), channel_id=1, source_target_pairs={{0,8},{4,12},{8,0},{12,4},{16,24},{20,28},{24,16},{28,20},{1,9},{5... | collective-permute-start | bytes 393224 | tf_op jit(solution)/shard_map/ppermute | solution.py:20
  3.7 8.0 %collective-permute-start.2 = (bf16[16,4096]{1,0:T(8,128)(2,1)}, bf16[16,4096]{1,0:T(8,128)(2,1)S(1)}, u32[]{:S(2)}, u32[]{:S(2)}) collective-permute-start(bf16[16,4096]{1,0:T(8,128)(2,1)} %refs_2_.1), channel_id=1, source_target_pairs={{0,16},{4,20},{8,24},{12,28},{16,0},{20,4},{24,8},{28,12},{1,17},{... | collective-permute-start | bytes 393224 | tf_op jit(solution)/shard_map/ppermute | solution.py:20
  5.2 6.5 %collective-permute-start.5 = (bf16[16,4096]{1,0:T(8,128)(2,1)}, bf16[16,4096]{1,0:T(8,128)(2,1)S(1)}, u32[]{:S(2)}, u32[]{:S(2)}) collective-permute-start(bf16[16,4096]{1,0:T(8,128)(2,1)} %refs_2_.1), channel_id=1, source_target_pairs={{0,24},{4,28},{8,16},{12,20},{16,8},{20,12},{24,0},{28,4},{1,25},{... | collective-permute-start | bytes 393224 | tf_op jit(solution)/shard_map/ppermute | solution.py:20
  5.2 11.7 %collective-permute-start.4 = (bf16[16,4096]{1,0:T(8,128)(2,1)}, bf16[16,4096]{1,0:T(8,128)(2,1)S(1)}, u32[]{:S(2)}, u32[]{:S(2)}) collective-permute-start(bf16[16,4096]{1,0:T(8,128)(2,1)} %refs_2_.1), channel_id=1, source_target_pairs={{0,4},{4,0},{8,12},{12,8},{16,20},{20,16},{24,28},{28,24},{1,5},{5... | collective-permute-start | bytes 393224 | tf_op jit(solution)/shard_map/ppermute | solution.py:20
  7.9 9.1 %collective-permute-start.1 = (bf16[16,4096]{1,0:T(8,128)(2,1)S(1)}, bf16[16,4096]{1,0:T(8,128)(2,1)S(1)}, u32[]{:S(2)}, u32[]{:S(2)}) collective-permute-start(bf16[16,4096]{1,0:T(8,128)(2,1)S(1)} %collective-permute-done.refs_0_), channel_id=1, source_target_pairs={{0,4},{4,0},{8,12},{12,8},{16,20},{20,16},{24,28},{28,24},{1,5},{5... | collective-permute-start | bytes 393224 | tf_op jit(solution)/shard_map/ppermute | solution.py:20
  11.7 5.3 %collective-permute-start.3 = (bf16[16,4096]{1,0:T(8,128)(2,1)S(1)}, bf16[16,4096]{1,0:T(8,128)(2,1)S(1)}, u32[]{:S(2)}, u32[]{:S(2)}) collective-permute-start(bf16[16,4096]{1,0:T(8,128)(2,1)S(1)} %collective-permute-done.2.refs_1_), channel_id=1, source_target_pairs={{0,4},{4,0},{8,12},{12,8},{16,20},{20,16},{24,28},{28,24},{1,5},{5... | collective-permute-start | bytes 393224 | tf_op jit(solution)/shard_map/ppermute | solution.py:20
  11.7 5.3 %collective-permute-start.6 = (bf16[16,4096]{1,0:T(8,128)(2,1)S(1)}, bf16[16,4096]{1,0:T(8,128)(2,1)S(1)}, u32[]{:S(2)}, u32[]{:S(2)}) collective-permute-start(bf16[16,4096]{1,0:T(8,128)(2,1)S(1)} %collective-permute-done.5.refs_3_), channel_id=1, source_target_pairs={{0,4},{4,0},{8,12},{12,8},{16,20},{20,16},{24,28},{28,24},{1,5},{5... | collective-permute-start | bytes 393224 | tf_op jit(solution)/shard_map/ppermute | solution.py:20
  12.2 4.6 %copy-start = (bf16[16,4096]{1,0:T(8,128)(2,1)S(1)}, bf16[16,4096]{1,0:T(8,128)(2,1)}, u32[]{:S(2)}) copy-start(bf16[16,4096]{1,0:T(8,128)(2,1)} %refs_2_.1) | copy-start | bytes 393220
  18.8 5.9 %collective-permute-start.7 = (f32[128,128]{1,0:T(8,128)S(1)}, f32[128,128]{1,0:T(8,128)S(1)}, u32[]{:S(2)}, u32[]{:S(2)}) collective-permute-start(f32[128,128]{1,0:T(8,128)S(1)} %get-tuple-element.26), channel_id=1, source_target_pairs={{0,1},{1,0},{2,3},{3,2},{4,5},{5,4},{6,7},{7,6},{8,9},{9,8},{10,11... | collective-permute-start | bytes 196616 | tf_op jit(solution)/shard_map/ppermute | solution.py:20
  20.5 7.5 %collective-permute-start.8 = (f32[128,128]{1,0:T(8,128)S(1)}, f32[128,128]{1,0:T(8,128)S(1)}, u32[]{:S(2)}, u32[]{:S(2)}) collective-permute-start(f32[128,128]{1,0:T(8,128)S(1)} %get-tuple-element.27), channel_id=1, source_target_pairs={{0,2},{1,3},{2,0},{3,1},{4,6},{5,7},{6,4},{7,5},{8,10},{9,11},{10,... | collective-permute-start | bytes 196616 | tf_op jit(solution)/shard_map/ppermute | solution.py:20
  23.0 6.2 %collective-permute-start.9 = (f32[128,128]{1,0:T(8,128)S(1)}, f32[128,128]{1,0:T(8,128)S(1)}, u32[]{:S(2)}, u32[]{:S(2)}) collective-permute-start(f32[128,128]{1,0:T(8,128)S(1)} %get-tuple-element.28), channel_id=1, source_target_pairs={{0,3},{1,2},{2,1},{3,0},{4,7},{5,6},{6,5},{7,4},{8,11},{9,10},{10,... | collective-permute-start | bytes 196616 | tf_op jit(solution)/shard_map/ppermute | solution.py:20
  29.3 4.5 %collective-permute-start.10 = (bf16[144,128]{1,0:T(8,128)(2,1)S(1)}, bf16[144,128]{1,0:T(8,128)(2,1)S(1)}, u32[]{:S(2)}, u32[]{:S(2)}) collective-permute-start(bf16[144,128]{1,0:T(8,128)(2,1)S(1)} %weigh.1.refs_0_), channel_id=1, source_target_pairs={{0,1},{1,0},{2,3},{3,2},{4,5},{5,4},{6,7},{7,6},{8,9},{9,8},{10,11... | collective-permute-start | bytes 110600 | tf_op jit(solution)/shard_map/ppermute | solution.py:20
  30.1 4.9 %collective-permute-start.11 = (bf16[144,128]{1,0:T(8,128)(2,1)S(1)}, bf16[144,128]{1,0:T(8,128)(2,1)S(1)}, u32[]{:S(2)}, u32[]{:S(2)}) collective-permute-start(bf16[144,128]{1,0:T(8,128)(2,1)S(1)} %weigh.1.refs_0_), channel_id=1, source_target_pairs={{0,2},{1,3},{2,0},{3,1},{4,6},{5,7},{6,4},{7,5},{8,10},{9,11},{10,... | collective-permute-start | bytes 110600 | tf_op jit(solution)/shard_map/ppermute | solution.py:20
  31.8 5.8 %collective-permute-start.12 = (bf16[144,128]{1,0:T(8,128)(2,1)S(1)}, bf16[144,128]{1,0:T(8,128)(2,1)S(1)}, u32[]{:S(2)}, u32[]{:S(2)}) collective-permute-start(bf16[144,128]{1,0:T(8,128)(2,1)S(1)} %weigh.1.refs_0_), channel_id=1, source_target_pairs={{0,3},{1,2},{2,1},{3,0},{4,7},{5,6},{6,5},{7,4},{8,11},{9,10},{10,... | collective-permute-start | bytes 110600 | tf_op jit(solution)/shard_map/ppermute | solution.py:20
  38.3 1.6 %collective-permute-start.14 = (bf16[32,4096]{1,0:T(8,128)(2,1)S(1)}, bf16[32,4096]{1,0:T(8,128)(2,1)S(1)}, u32[]{:S(2)}, u32[]{:S(2)}) collective-permute-start(bf16[32,4096]{1,0:T(8,128)(2,1)S(1)} %get-tuple-element.33), channel_id=1, source_target_pairs={{0,4},{4,0},{8,12},{12,8},{16,20},{20,16},{24,28},{28,24},{1,5},{5... | collective-permute-start | bytes 786440 | tf_op jit(solution)/shard_map/ppermute | solution.py:20
  38.4 3.7 %collective-permute-start.13 = (bf16[32,4096]{1,0:T(8,128)(2,1)S(1)}, bf16[32,4096]{1,0:T(8,128)(2,1)S(1)}, u32[]{:S(2)}, u32[]{:S(2)}) collective-permute-start(bf16[32,4096]{1,0:T(8,128)(2,1)S(1)} %get-tuple-element.31), channel_id=1, source_target_pairs={{0,4},{4,0},{8,12},{12,8},{16,20},{20,16},{24,28},{28,24},{1,5},{5... | collective-permute-start | bytes 786440 | tf_op jit(solution)/shard_map/ppermute | solution.py:20
  39.9 6.2 %collective-permute-start.15 = (bf16[16,4096]{1,0:T(8,128)(2,1)S(1)}, bf16[16,4096]{1,0:T(8,128)(2,1)S(1)}, u32[]{:S(2)}, u32[]{:S(2)}) collective-permute-start(bf16[16,4096]{1,0:T(8,128)(2,1)S(1)} %get-tuple-element.34), channel_id=1, source_target_pairs={{0,8},{4,12},{8,0},{12,4},{16,24},{20,28},{24,16},{28,20},{1,9},{5... | collective-permute-start | bytes 393224 | tf_op jit(solution)/shard_map/ppermute | solution.py:20
  41.2 6.5 %collective-permute-start.16 = (bf16[16,4096]{1,0:T(8,128)(2,1)S(1)}, bf16[16,4096]{1,0:T(8,128)(2,1)S(1)}, u32[]{:S(2)}, u32[]{:S(2)}) collective-permute-start(bf16[16,4096]{1,0:T(8,128)(2,1)S(1)} %get-tuple-element.35), channel_id=1, source_target_pairs={{0,16},{4,20},{8,24},{12,28},{16,0},{20,4},{24,8},{28,12},{1,17},{... | collective-permute-start | bytes 393224 | tf_op jit(solution)/shard_map/ppermute | solution.py:20
  42.1 7.2 %collective-permute-start.17 = (bf16[16,4096]{1,0:T(8,128)(2,1)S(1)}, bf16[16,4096]{1,0:T(8,128)(2,1)S(1)}, u32[]{:S(2)}, u32[]{:S(2)}) collective-permute-start(bf16[16,4096]{1,0:T(8,128)(2,1)S(1)} %get-tuple-element.36), channel_id=1, source_target_pairs={{0,24},{4,28},{8,16},{12,20},{16,8},{20,12},{24,0},{28,4},{1,25},{... | collective-permute-start | bytes 393224 | tf_op jit(solution)/shard_map/ppermute | solution.py:20

commit v3 on v2

--- a/solution.py
+++ b/solution.py
@@ -149,8 +149,8 @@
         lines_all[span, :] = value
         square_all[span, :] = (-0.5 * wide * wide).astype(BF16)
     lanes = outs[0].shape[1]
-    total = lax.dot_general(weighted[lanes:, :], lines_all[...], NT, preferred_element_type=F32) + lax.dot_general(
-        quadratic[lanes:, :], square_all[...], NT, preferred_element_type=F32
+    total = lax.dot_general(weighted[2 * lanes :, :], lines_all[...], NT, preferred_element_type=F32) + lax.dot_general(
+        quadratic[2 * lanes :, :], square_all[...], NT, preferred_element_type=F32
     )
     for j, out in enumerate(outs):
         out[...] = total[j * lanes : (j + 1) * lanes, :].T
@@ -162,29 +162,30 @@
     slots = weighted.shape[0]
     return pl.pallas_call(
         functools.partial(score_kernel, len(proj)),
-        out_shape=tuple(pltpu.VMEM((orients, slots // parts), F32) for _ in range(parts - 1))
+        out_shape=tuple(pltpu.VMEM((orients, slots // parts), F32) for _ in range(parts - 2))
         + (pltpu.VMEM((orients, pixels), BF16),) * 2,
         in_specs=[VMEM] * (len(proj) + 4),
-        out_specs=(VMEM,) * (parts + 1),
+        out_specs=(VMEM,) * parts,
         compiler_params=params(12),
         cost_estimate=cost(4 * orients * slots * pixels, 4 * slots * pixels),
         name="score",
     )(*proj, lines, square, weighted, quadratic)
 
 
-def own_kernel(lines, square, weighted, quadratic, out):
+def own_kernel(base, lines, square, weighted, quadratic, out):
     lanes = out.shape[1]
-    total = lax.dot_general(weighted[:lanes, :], lines[...], NT, preferred_element_type=F32) + lax.dot_general(
-        quadratic[:lanes, :], square[...], NT, preferred_element_type=F32
+    held = slice(base * lanes, (base + 1) * lanes)
+    total = lax.dot_general(weighted[held, :], lines[...], NT, preferred_element_type=F32) + lax.dot_general(
+        quadratic[held, :], square[...], NT, preferred_element_type=F32
     )
     out[...] = total.T
 
 
-def own_score(parts, lines, square, weighted, quadratic):
+def own_score(parts, base, lines, square, weighted, quadratic):
     orients, pixels = lines.shape
     lanes = weighted.shape[0] // parts
     return pl.pallas_call(
-        own_kernel,
+        functools.partial(own_kernel, base),
         out_shape=pltpu.VMEM((orients, lanes), F32),
         in_specs=[VMEM] * 4,
         out_specs=VMEM,
@@ -331,9 +332,11 @@
     lines, square = squares([far[k] for k in lead])
     *chunks, lines, square = score(pix, [near[k] for k in lead], lines, square, weighted, quadratic)
     pieces = []
-    for j in range(1, pix):
-        pieces.append(swap(chunks[j - 1], "pix", pix, j))
-    pieces.insert(0, own_score(pix, lines, square, weighted, quadratic))
+    for j in range(2, pix):
+        pieces.append(swap(chunks[j - 2], "pix", pix, j))
+    beside = own_score(pix, 1, lines, square, weighted, quadratic)
+    pieces.append(swap(beside, "pix", pix, 1))
+    pieces.insert(0, own_score(pix, 0, lines, square, weighted, quadratic))
     weights = weigh(pieces, prior, counts)
     parts = [weights]
     for j in range(1, pix):

time: 50.2 us -> 50.4 us (level)
    pallas_call x1 -> x2, Pallas kernels: 0.77 us -> 1.54 us  [own_score(): pl.pallas_call(functools.partial(own_kernel, base), out_shape=pltpu.VMEM(...]
    pallas_call x1, Pallas kernels: 1.86 us -> 1.32 us  [score(): pl.pallas_call(functools.partial(score_kernel, len(proj)), out_shape=tupl...]
where the time goes in v3:
time: 50.4 us; the launch traced here: 50.3 us
  waiting for transfers between devices  20.9 us (41%)
  starting transfers between devices  18.2 us (36%)
  Pallas kernels  9.23 us (18%)
  between operations  1.4 us (3%)
  local copies, waits for them, and re-layouts  0.58 us (1%)
    ppermute x18, waiting for transfers between devices, swap(): out = lax.ppermute(value, axis, [(i, i ^ k) for i in range(size)])  20.9 us
    ppermute x18, starting transfers between devices, swap(): out = lax.ppermute(value, axis, [(i, i ^ k) for i in range(size)])  18.2 us
    pallas_call x1, Pallas kernels, prepare(): pl.pallas_call(functools.partial(prepare_kernel, order, rows), out_shape=...  4.55 us
    pallas_call x2, Pallas kernels, own_score(): pl.pallas_call(functools.partial(own_kernel, base), out_shape=pltpu.VMEM(...  1.54 us
    pallas_call x1, Pallas kernels, score(): pl.pallas_call(functools.partial(score_kernel, len(proj)), out_shape=tupl...  1.32 us
  transfers between devices with their start and end apart: 18, of which 10 were waited for; matrix products, arithmetic and copies ran while one was open for 1% of the time, Pallas kernels for 11%

profile of v3, /device:TPU:0, one launch (start us, length us, event | category | flops | bytes accessed | tf_op | source)
XLA Modules:
  0.0 50.3 jit_solution(792246234855659954)
XLA Ops:
  0.6 3.0 %collective-permute-start = (bf16[16,4096]{1,0:T(8,128)(2,1)}, bf16[16,4096]{1,0:T(8,128)(2,1)S(1)}, u32[]{:S(2)}, u32[]{:S(2)}) collective-permute-start(bf16[16,4096]{1,0:T(8,128)(2,1)} %refs_2_.1), channel_id=1, source_target_pairs={{0,8},{4,12},{8,0},{12,4},{16,24},{20,28},{24,16},{28,20},{1,9},{5... | collective-permute-start | bytes 393224 | tf_op jit(solution)/shard_map/ppermute | solution.py:20
  3.7 1.5 %collective-permute-start.2 = (bf16[16,4096]{1,0:T(8,128)(2,1)}, bf16[16,4096]{1,0:T(8,128)(2,1)S(1)}, u32[]{:S(2)}, u32[]{:S(2)}) collective-permute-start(bf16[16,4096]{1,0:T(8,128)(2,1)} %refs_2_.1), channel_id=1, source_target_pairs={{0,16},{4,20},{8,24},{12,28},{16,0},{20,4},{24,8},{28,12},{1,17},{... | collective-permute-start | bytes 393224 | tf_op jit(solution)/shard_map/ppermute | solution.py:20
  5.2 2.7 %collective-permute-done.refs_0_ = bf16[16,4096]{1,0:T(8,128)(2,1)S(1)} collective-permute-done((bf16[16,4096]{1,0:T(8,128)(2,1)}, bf16[16,4096]{1,0:T(8,128)(2,1)S(1)}, u32[]{:S(2)}, u32[]{:S(2)}) %collective-permute-start) | collective-permute-done | bytes 131104 | tf_op jit(solution)/shard_map/ppermute | solution.py:20
  7.9 3.8 %collective-permute-done.2.refs_1_ = bf16[16,4096]{1,0:T(8,128)(2,1)S(1)} collective-permute-done((bf16[16,4096]{1,0:T(8,128)(2,1)}, bf16[16,4096]{1,0:T(8,128)(2,1)S(1)}, u32[]{:S(2)}, u32[]{:S(2)}) %collective-permute-start.2) | collective-permute-done | bytes 131104 | tf_op jit(solution)/shard_map/ppermute | solution.py:20
  12.2 4.5 %prepare.1 = (bf16[512,4096]{1,0:T(8,128)(2,1)S(1)}, bf16[512,4096]{1,0:T(8,128)(2,1)S(1)}, f32[128,128]{1,0:T(8,128)S(1)}) custom-call(bf16[512,4096]{1,0:T(8,128)(2,1)} %particles.1, bf16[512,4096]{1,0:T(8,128)(2,1)} %ctf.1, f32[1,4096]{1,0:T(1,128)} %bitcast.5, s32[1,128]{1,0:T(1,128)} %bitcast.6, f32[1,5]{1,0:T(1,128)} %bitcast.7), custom_call_target="tpu_custom_call" | custom-call | flops 33554432 | bytes 16777216 | tf_op jit(solution)/shard_map/prepare/pallas_call | solution.py:85
  16.9 1.3 %score.1 = (f32[128,128]{1,0:T(8,128)S(1)}, f32[128,128]{1,0:T(8,128)S(1)}, bf16[128,4096]{1,0:T(8,128)(2,1)S(1)}, bf16[128,4096]{1,0:T(8,128)(2,1)S(1)}) custom-call(bf16[16,4096]{1,0:T(8,128)(2,1)S(1)} %collective-permute-done.1.refs_0_, bf16[16,4096]{1,0:T(8,128)(2,1)S(1)} %collective-permute-done.3.refs_1_, ...), custom_call_target="tpu_custom_call" | custom-call | flops 1073741824 | bytes 8388608 | tf_op jit(solution)/shard_map/score/pallas_call | solution.py:163
  18.3 0.8 %own_score.3 = f32[128,128]{1,0:T(8,128)S(1)} custom-call(bf16[128,4096]{1,0:T(8,128)(2,1)S(1)} %get-tuple-element.23.lines, bf16[128,4096]{1,0:T(8,128)(2,1)S(1)} %get-tuple-element.24.square, bf16[512,4096]{1,0:T(8,128)(2,1)S(1)} %get-tuple-element.21.refs_6_.weighted.refs_4_, bf16[512,4096]{1,0:T(8,128)(2,1)S(1)} %get-tuple-element.22.refs_7_.quadratic), custom_call_target="tpu_custom_call" | custom-call | flops 268435456 | bytes 2097152 | tf_op jit(solution)/shard_map/own_score/pallas_call | solution.py:187
  19.0 1.6 %collective-permute-start.9 = (f32[128,128]{1,0:T(8,128)S(1)}, f32[128,128]{1,0:T(8,128)S(1)}, u32[]{:S(2)}, u32[]{:S(2)}) collective-permute-start(f32[128,128]{1,0:T(8,128)S(1)} %own_score.3), channel_id=1, source_target_pairs={{0,1},{1,0},{2,3},{3,2},{4,5},{5,4},{6,7},{7,6},{8,9},{9,8},{10,11... | collective-permute-start | bytes 196616 | tf_op jit(solution)/shard_map/ppermute | solution.py:20
  20.7 2.6 %collective-permute-start.7 = (f32[128,128]{1,0:T(8,128)S(1)}, f32[128,128]{1,0:T(8,128)S(1)}, u32[]{:S(2)}, u32[]{:S(2)}) collective-permute-start(f32[128,128]{1,0:T(8,128)S(1)} %get-tuple-element.25), channel_id=1, source_target_pairs={{0,2},{1,3},{2,0},{3,1},{4,6},{5,7},{6,4},{7,5},{8,10},{9,11},{10,... | collective-permute-start | bytes 196616 | tf_op jit(solution)/shard_map/ppermute | solution.py:20
  24.2 0.8 %own_score.2.refs_0_ = f32[128,128]{1,0:T(8,128)S(1)} custom-call(bf16[128,4096]{1,0:T(8,128)(2,1)S(1)} %get-tuple-element.23.lines, bf16[128,4096]{1,0:T(8,128)(2,1)S(1)} %get-tuple-element.24.square, bf16[512,4096]{1,0:T(8,128)(2,1)S(1)} %get-tuple-element.21.refs_6_.weighted.refs_4_, bf16[512,4096]{1,0:T(8,128)(2,1)S(1)} %get-tuple-element.22.refs_7_.quadratic), custom_call_target="tpu_custom_call" | custom-call | flops 268435456 | bytes 2097152 | tf_op jit(solution)/shard_map/own_score/pallas_call | solution.py:187
  24.9 3.2 %collective-permute-done.7.refs_1_ = f32[128,128]{1,0:T(8,128)S(1)} collective-permute-done((f32[128,128]{1,0:T(8,128)S(1)}, f32[128,128]{1,0:T(8,128)S(1)}, u32[]{:S(2)}, u32[]{:S(2)}) %collective-permute-start.7) | collective-permute-done | bytes 65568 | tf_op jit(solution)/shard_map/ppermute | solution.py:20
  28.1 1.3 %collective-permute-done.8.refs_2_ = f32[128,128]{1,0:T(8,128)S(1)} collective-permute-done((f32[128,128]{1,0:T(8,128)S(1)}, f32[128,128]{1,0:T(8,128)S(1)}, u32[]{:S(2)}, u32[]{:S(2)}) %collective-permute-start.8) | collective-permute-done | bytes 65568 | tf_op jit(solution)/shard_map/ppermute | solution.py:20
  29.5 0.8 %collective-permute-start.10 = (bf16[144,128]{1,0:T(8,128)(2,1)S(1)}, bf16[144,128]{1,0:T(8,128)(2,1)S(1)}, u32[]{:S(2)}, u32[]{:S(2)}) collective-permute-start(bf16[144,128]{1,0:T(8,128)(2,1)S(1)} %weigh.1.refs_0_), channel_id=1, source_target_pairs={{0,1},{1,0},{2,3},{3,2},{4,5},{5,4},{6,7},{7,6},{8,9},{9,8},{10,11... | collective-permute-start | bytes 110600 | tf_op jit(solution)/shard_map/ppermute | solution.py:20
  30.3 1.7 %collective-permute-start.11 = (bf16[144,128]{1,0:T(8,128)(2,1)S(1)}, bf16[144,128]{1,0:T(8,128)(2,1)S(1)}, u32[]{:S(2)}, u32[]{:S(2)}) collective-permute-start(bf16[144,128]{1,0:T(8,128)(2,1)S(1)} %weigh.1.refs_0_), channel_id=1, source_target_pairs={{0,2},{1,3},{2,0},{3,1},{4,6},{5,7},{6,4},{7,5},{8,10},{9,11},{10,... | collective-permute-start | bytes 110600 | tf_op jit(solution)/shard_map/ppermute | solution.py:20
  32.0 2.0 %collective-permute-start.12 = (bf16[144,128]{1,0:T(8,128)(2,1)S(1)}, bf16[144,128]{1,0:T(8,128)(2,1)S(1)}, u32[]{:S(2)}, u32[]{:S(2)}) collective-permute-start(bf16[144,128]{1,0:T(8,128)(2,1)S(1)} %weigh.1.refs_0_), channel_id=1, source_target_pairs={{0,3},{1,2},{2,1},{3,0},{4,7},{5,6},{6,5},{7,4},{8,11},{9,10},{10,... | collective-permute-start | bytes 110600 | tf_op jit(solution)/shard_map/ppermute | solution.py:20
  34.0 1.2 %collective-permute-done.11.refs_2_ = bf16[144,128]{1,0:T(8,128)(2,1)S(1)} collective-permute-done((bf16[144,128]{1,0:T(8,128)(2,1)S(1)}, bf16[144,128]{1,0:T(8,128)(2,1)S(1)}, u32[]{:S(2)}, u32[]{:S(2)}) %collective-permute-start.11) | collective-permute-done | bytes 36896 | tf_op jit(solution)/shard_map/ppermute | solution.py:20
  35.2 2.6 %collective-permute-done.12.refs_3_ = bf16[144,128]{1,0:T(8,128)(2,1)S(1)} collective-permute-done((bf16[144,128]{1,0:T(8,128)(2,1)S(1)}, bf16[144,128]{1,0:T(8,128)(2,1)S(1)}, u32[]{:S(2)}, u32[]{:S(2)}) %collective-permute-start.12) | collective-permute-done | bytes 36896 | tf_op jit(solution)/shard_map/ppermute | solution.py:20
  39.1 1.0 %collective-permute-done.14.got = bf16[32,4096]{1,0:T(8,128)(2,1)S(1)} collective-permute-done((bf16[32,4096]{1,0:T(8,128)(2,1)S(1)}, bf16[32,4096]{1,0:T(8,128)(2,1)S(1)}, u32[]{:S(2)}, u32[]{:S(2)}) %collective-permute-start.14) | collective-permute-done | bytes 262176 | tf_op jit(solution)/shard_map/ppermute | solution.py:20
  40.2 1.3 %collective-permute-start.15 = (bf16[16,4096]{1,0:T(8,128)(2,1)S(1)}, bf16[16,4096]{1,0:T(8,128)(2,1)S(1)}, u32[]{:S(2)}, u32[]{:S(2)}) collective-permute-start(bf16[16,4096]{1,0:T(8,128)(2,1)S(1)} %get-tuple-element.32), channel_id=1, source_target_pairs={{0,8},{4,12},{8,0},{12,4},{16,24},{20,28},{24,16},{28,20},{1,9},{5... | collective-permute-start | bytes 393224 | tf_op jit(solution)/shard_map/ppermute | solution.py:20
  41.4 0.8 %collective-permute-start.16 = (bf16[16,4096]{1,0:T(8,128)(2,1)S(1)}, bf16[16,4096]{1,0:T(8,128)(2,1)S(1)}, u32[]{:S(2)}, u32[]{:S(2)}) collective-permute-start(bf16[16,4096]{1,0:T(8,128)(2,1)S(1)} %get-tuple-element.33), channel_id=1, source_target_pairs={{0,16},{4,20},{8,24},{12,28},{16,0},{20,4},{24,8},{28,12},{1,17},{... | collective-permute-start | bytes 393224 | tf_op jit(solution)/shard_map/ppermute | solution.py:20
  42.3 1.5 %collective-permute-start.17 = (bf16[16,4096]{1,0:T(8,128)(2,1)S(1)}, bf16[16,4096]{1,0:T(8,128)(2,1)S(1)}, u32[]{:S(2)}, u32[]{:S(2)}) collective-permute-start(bf16[16,4096]{1,0:T(8,128)(2,1)S(1)} %get-tuple-element.34), channel_id=1, source_target_pairs={{0,24},{4,28},{8,16},{12,20},{16,8},{20,12},{24,0},{28,4},{1,25},{... | collective-permute-start | bytes 393224 | tf_op jit(solution)/shard_map/ppermute | solution.py:20
  44.4 1.9 %collective-permute-done.15.refs_0_ = bf16[16,4096]{1,0:T(8,128)(2,1)S(1)} collective-permute-done((bf16[16,4096]{1,0:T(8,128)(2,1)S(1)}, bf16[16,4096]{1,0:T(8,128)(2,1)S(1)}, u32[]{:S(2)}, u32[]{:S(2)}) %collective-permute-start.15) | collective-permute-done | bytes 131104 | tf_op jit(solution)/shard_map/ppermute | solution.py:20
  46.3 1.6 %collective-permute-done.16.refs_1_ = bf16[16,4096]{1,0:T(8,128)(2,1)S(1)} collective-permute-done((bf16[16,4096]{1,0:T(8,128)(2,1)S(1)}, bf16[16,4096]{1,0:T(8,128)(2,1)S(1)}, u32[]{:S(2)}, u32[]{:S(2)}) %collective-permute-start.16) | collective-permute-done | bytes 131104 | tf_op jit(solution)/shard_map/ppermute | solution.py:20
  47.9 1.6 %collective-permute-done.17.refs_2_ = bf16[16,4096]{1,0:T(8,128)(2,1)S(1)} collective-permute-done((bf16[16,4096]{1,0:T(8,128)(2,1)S(1)}, bf16[16,4096]{1,0:T(8,128)(2,1)S(1)}, u32[]{:S(2)}, u32[]{:S(2)}) %collective-permute-start.17) | collective-permute-done | bytes 131104 | tf_op jit(solution)/shard_map/ppermute | solution.py:20
  (25 shorter events, 3.7 us)
Async XLA Ops:
  0.6 7.2 %collective-permute-start = (bf16[16,4096]{1,0:T(8,128)(2,1)}, bf16[16,4096]{1,0:T(8,128)(2,1)S(1)}, u32[]{:S(2)}, u32[]{:S(2)}) collective-permute-start(bf16[16,4096]{1,0:T(8,128)(2,1)} %refs_2_.1), channel_id=1, source_target_pairs={{0,8},{4,12},{8,0},{12,4},{16,24},{20,28},{24,16},{28,20},{1,9},{5... | collective-permute-start | bytes 393224 | tf_op jit(solution)/shard_map/ppermute | solution.py:20
  3.7 8.0 %collective-permute-start.2 = (bf16[16,4096]{1,0:T(8,128)(2,1)}, bf16[16,4096]{1,0:T(8,128)(2,1)S(1)}, u32[]{:S(2)}, u32[]{:S(2)}) collective-permute-start(bf16[16,4096]{1,0:T(8,128)(2,1)} %refs_2_.1), channel_id=1, source_target_pairs={{0,16},{4,20},{8,24},{12,28},{16,0},{20,4},{24,8},{28,12},{1,17},{... | collective-permute-start | bytes 393224 | tf_op jit(solution)/shard_map/ppermute | solution.py:20
  5.2 6.5 %collective-permute-start.5 = (bf16[16,4096]{1,0:T(8,128)(2,1)}, bf16[16,4096]{1,0:T(8,128)(2,1)S(1)}, u32[]{:S(2)}, u32[]{:S(2)}) collective-permute-start(bf16[16,4096]{1,0:T(8,128)(2,1)} %refs_2_.1), channel_id=1, source_target_pairs={{0,24},{4,28},{8,16},{12,20},{16,8},{20,12},{24,0},{28,4},{1,25},{... | collective-permute-start | bytes 393224 | tf_op jit(solution)/shard_map/ppermute | solution.py:20
  5.2 11.7 %collective-permute-start.4 = (bf16[16,4096]{1,0:T(8,128)(2,1)}, bf16[16,4096]{1,0:T(8,128)(2,1)S(1)}, u32[]{:S(2)}, u32[]{:S(2)}) collective-permute-start(bf16[16,4096]{1,0:T(8,128)(2,1)} %refs_2_.1), channel_id=1, source_target_pairs={{0,4},{4,0},{8,12},{12,8},{16,20},{20,16},{24,28},{28,24},{1,5},{5... | collective-permute-start | bytes 393224 | tf_op jit(solution)/shard_map/ppermute | solution.py:20
  7.9 9.1 %collective-permute-start.1 = (bf16[16,4096]{1,0:T(8,128)(2,1)S(1)}, bf16[16,4096]{1,0:T(8,128)(2,1)S(1)}, u32[]{:S(2)}, u32[]{:S(2)}) collective-permute-start(bf16[16,4096]{1,0:T(8,128)(2,1)S(1)} %collective-permute-done.refs_0_), channel_id=1, source_target_pairs={{0,4},{4,0},{8,12},{12,8},{16,20},{20,16},{24,28},{28,24},{1,5},{5... | collective-permute-start | bytes 393224 | tf_op jit(solution)/shard_map/ppermute | solution.py:20
  11.7 5.3 %collective-permute-start.3 = (bf16[16,4096]{1,0:T(8,128)(2,1)S(1)}, bf16[16,4096]{1,0:T(8,128)(2,1)S(1)}, u32[]{:S(2)}, u32[]{:S(2)}) collective-permute-start(bf16[16,4096]{1,0:T(8,128)(2,1)S(1)} %collective-permute-done.2.refs_1_), channel_id=1, source_target_pairs={{0,4},{4,0},{8,12},{12,8},{16,20},{20,16},{24,28},{28,24},{1,5},{5... | collective-permute-start | bytes 393224 | tf_op jit(solution)/shard_map/ppermute | solution.py:20
  11.7 5.3 %collective-permute-start.6 = (bf16[16,4096]{1,0:T(8,128)(2,1)S(1)}, bf16[16,4096]{1,0:T(8,128)(2,1)S(1)}, u32[]{:S(2)}, u32[]{:S(2)}) collective-permute-start(bf16[16,4096]{1,0:T(8,128)(2,1)S(1)} %collective-permute-done.5.refs_3_), channel_id=1, source_target_pairs={{0,4},{4,0},{8,12},{12,8},{16,20},{20,16},{24,28},{28,24},{1,5},{5... | collective-permute-start | bytes 393224 | tf_op jit(solution)/shard_map/ppermute | solution.py:20
  12.2 4.6 %copy-start = (bf16[16,4096]{1,0:T(8,128)(2,1)S(1)}, bf16[16,4096]{1,0:T(8,128)(2,1)}, u32[]{:S(2)}) copy-start(bf16[16,4096]{1,0:T(8,128)(2,1)} %refs_2_.1) | copy-start | bytes 393220
  19.0 5.9 %collective-permute-start.9 = (f32[128,128]{1,0:T(8,128)S(1)}, f32[128,128]{1,0:T(8,128)S(1)}, u32[]{:S(2)}, u32[]{:S(2)}) collective-permute-start(f32[128,128]{1,0:T(8,128)S(1)} %own_score.3), channel_id=1, source_target_pairs={{0,1},{1,0},{2,3},{3,2},{4,5},{5,4},{6,7},{7,6},{8,9},{9,8},{10,11... | collective-permute-start | bytes 196616 | tf_op jit(solution)/shard_map/ppermute | solution.py:20
  20.7 7.5 %collective-permute-start.7 = (f32[128,128]{1,0:T(8,128)S(1)}, f32[128,128]{1,0:T(8,128)S(1)}, u32[]{:S(2)}, u32[]{:S(2)}) collective-permute-start(f32[128,128]{1,0:T(8,128)S(1)} %get-tuple-element.25), channel_id=1, source_target_pairs={{0,2},{1,3},{2,0},{3,1},{4,6},{5,7},{6,4},{7,5},{8,10},{9,11},{10,... | collective-permute-start | bytes 196616 | tf_op jit(solution)/shard_map/ppermute | solution.py:20
  23.3 6.2 %collective-permute-start.8 = (f32[128,128]{1,0:T(8,128)S(1)}, f32[128,128]{1,0:T(8,128)S(1)}, u32[]{:S(2)}, u32[]{:S(2)}) collective-permute-start(f32[128,128]{1,0:T(8,128)S(1)} %get-tuple-element.26), channel_id=1, source_target_pairs={{0,3},{1,2},{2,1},{3,0},{4,7},{5,6},{6,5},{7,4},{8,11},{9,10},{10,... | collective-permute-start | bytes 196616 | tf_op jit(solution)/shard_map/ppermute | solution.py:20
  29.5 4.5 %collective-permute-start.10 = (bf16[144,128]{1,0:T(8,128)(2,1)S(1)}, bf16[144,128]{1,0:T(8,128)(2,1)S(1)}, u32[]{:S(2)}, u32[]{:S(2)}) collective-permute-start(bf16[144,128]{1,0:T(8,128)(2,1)S(1)} %weigh.1.refs_0_), channel_id=1, source_target_pairs={{0,1},{1,0},{2,3},{3,2},{4,5},{5,4},{6,7},{7,6},{8,9},{9,8},{10,11... | collective-permute-start | bytes 110600 | tf_op jit(solution)/shard_map/ppermute | solution.py:20
  30.3 4.9 %collective-permute-start.11 = (bf16[144,128]{1,0:T(8,128)(2,1)S(1)}, bf16[144,128]{1,0:T(8,128)(2,1)S(1)}, u32[]{:S(2)}, u32[]{:S(2)}) collective-permute-start(bf16[144,128]{1,0:T(8,128)(2,1)S(1)} %weigh.1.refs_0_), channel_id=1, source_target_pairs={{0,2},{1,3},{2,0},{3,1},{4,6},{5,7},{6,4},{7,5},{8,10},{9,11},{10,... | collective-permute-start | bytes 110600 | tf_op jit(solution)/shard_map/ppermute | solution.py:20
  32.0 5.8 %collective-permute-start.12 = (bf16[144,128]{1,0:T(8,128)(2,1)S(1)}, bf16[144,128]{1,0:T(8,128)(2,1)S(1)}, u32[]{:S(2)}, u32[]{:S(2)}) collective-permute-start(bf16[144,128]{1,0:T(8,128)(2,1)S(1)} %weigh.1.refs_0_), channel_id=1, source_target_pairs={{0,3},{1,2},{2,1},{3,0},{4,7},{5,6},{6,5},{7,4},{8,11},{9,10},{10,... | collective-permute-start | bytes 110600 | tf_op jit(solution)/shard_map/ppermute | solution.py:20
  38.5 1.6 %collective-permute-start.14 = (bf16[32,4096]{1,0:T(8,128)(2,1)S(1)}, bf16[32,4096]{1,0:T(8,128)(2,1)S(1)}, u32[]{:S(2)}, u32[]{:S(2)}) collective-permute-start(bf16[32,4096]{1,0:T(8,128)(2,1)S(1)} %get-tuple-element.31), channel_id=1, source_target_pairs={{0,4},{4,0},{8,12},{12,8},{16,20},{20,16},{24,28},{28,24},{1,5},{5... | collective-permute-start | bytes 786440 | tf_op jit(solution)/shard_map/ppermute | solution.py:20
  38.6 3.7 %collective-permute-start.13 = (bf16[32,4096]{1,0:T(8,128)(2,1)S(1)}, bf16[32,4096]{1,0:T(8,128)(2,1)S(1)}, u32[]{:S(2)}, u32[]{:S(2)}) collective-permute-start(bf16[32,4096]{1,0:T(8,128)(2,1)S(1)} %get-tuple-element.29), channel_id=1, source_target_pairs={{0,4},{4,0},{8,12},{12,8},{16,20},{20,16},{24,28},{28,24},{1,5},{5... | collective-permute-start | bytes 786440 | tf_op jit(solution)/shard_map/ppermute | solution.py:20
  40.2 6.2 %collective-permute-start.15 = (bf16[16,4096]{1,0:T(8,128)(2,1)S(1)}, bf16[16,4096]{1,0:T(8,128)(2,1)S(1)}, u32[]{:S(2)}, u32[]{:S(2)}) collective-permute-start(bf16[16,4096]{1,0:T(8,128)(2,1)S(1)} %get-tuple-element.32), channel_id=1, source_target_pairs={{0,8},{4,12},{8,0},{12,4},{16,24},{20,28},{24,16},{28,20},{1,9},{5... | collective-permute-start | bytes 393224 | tf_op jit(solution)/shard_map/ppermute | solution.py:20
  41.4 6.5 %collective-permute-start.16 = (bf16[16,4096]{1,0:T(8,128)(2,1)S(1)}, bf16[16,4096]{1,0:T(8,128)(2,1)S(1)}, u32[]{:S(2)}, u32[]{:S(2)}) collective-permute-start(bf16[16,4096]{1,0:T(8,128)(2,1)S(1)} %get-tuple-element.33), channel_id=1, source_target_pairs={{0,16},{4,20},{8,24},{12,28},{16,0},{20,4},{24,8},{28,12},{1,17},{... | collective-permute-start | bytes 393224 | tf_op jit(solution)/shard_map/ppermute | solution.py:20
  42.3 7.2 %collective-permute-start.17 = (bf16[16,4096]{1,0:T(8,128)(2,1)S(1)}, bf16[16,4096]{1,0:T(8,128)(2,1)S(1)}, u32[]{:S(2)}, u32[]{:S(2)}) collective-permute-start(bf16[16,4096]{1,0:T(8,128)(2,1)S(1)} %get-tuple-element.34), channel_id=1, source_target_pairs={{0,24},{4,28},{8,16},{12,20},{16,8},{20,12},{24,0},{28,4},{1,25},{... | collective-permute-start | bytes 393224 | tf_op jit(solution)/shard_map/ppermute | solution.py:20

commit v4 on v3

--- a/solution.py
+++ b/solution.py
@@ -297,10 +297,22 @@
 
 
 def final_kernel(own, *refs):
-    total = own[...]
-    for piece in refs[:-1]:
-        total = total + piece[...].astype(F32)
-    refs[-1][...] = total
+    *pieces, out, held, sems = refs
+    copies = []
+    for i, span in enumerate(spans(own.shape[1])):
+        total = own[:, span]
+        for piece in pieces:
+            total = total + piece[:, span].astype(F32)
+        held[:, span] = total
+        copies.append(pltpu.make_async_copy(held.at[:, span], out.at[:, span], sems.at[i]))
+        copies[-1].start()
+    for copy in copies:
+        copy.wait()
+
+
+def spans(pixels):
+    wide = pixels // 4 if pixels % 512 == 0 else pixels
+    return [slice(c * wide, (c + 1) * wide) for c in range(pixels // wide)]
 
 
 def final(own, pieces):
@@ -308,7 +320,8 @@
         final_kernel,
         out_shape=jax.ShapeDtypeStruct(own.shape, F32),
         in_specs=[VMEM] * (len(pieces) + 1),
-        out_specs=VMEM,
+        out_specs=HBM,
+        scratch_shapes=[pltpu.VMEM(own.shape, F32), pltpu.SemaphoreType.DMA((len(spans(own.shape[1])),))],
         compiler_params=params(16),
         cost_estimate=cost(own.size * len(pieces), 4 * own.size * len(pieces)),
         name="final",

time: 50.4 us -> 50.4 us (level)
  no operation moved by 1% of the time
where the time goes in v4:
time: 50.4 us; the launch traced here: 50.3 us
  waiting for transfers between devices  20.9 us (41%)
  starting transfers between devices  18.2 us (36%)
  Pallas kernels  9.22 us (18%)
  between operations  1.4 us (3%)
  local copies, waits for them, and re-layouts  0.58 us (1%)
    ppermute x18, waiting for transfers between devices, swap(): out = lax.ppermute(value, axis, [(i, i ^ k) for i in range(size)])  20.9 us
    ppermute x18, starting transfers between devices, swap(): out = lax.ppermute(value, axis, [(i, i ^ k) for i in range(size)])  18.2 us
    pallas_call x1, Pallas kernels, prepare(): pl.pallas_call(functools.partial(prepare_kernel, order, rows), out_shape=...  4.55 us
    pallas_call x2, Pallas kernels, own_score(): pl.pallas_call(functools.partial(own_kernel, base), out_shape=pltpu.VMEM(...  1.54 us
    pallas_call x1, Pallas kernels, score(): pl.pallas_call(functools.partial(score_kernel, len(proj)), out_shape=tupl...  1.32 us
  transfers between devices with their start and end apart: 18, of which 10 were waited for; matrix products, arithmetic and copies ran while one was open for 1% of the time, Pallas kernels for 11%

profile of v4, /device:TPU:0, one launch (start us, length us, event | category | flops | bytes accessed | tf_op | source)
XLA Modules:
  0.0 50.3 jit_solution(16463887059976867716)
XLA Ops:
  0.6 3.0 %collective-permute-start = (bf16[16,4096]{1,0:T(8,128)(2,1)}, bf16[16,4096]{1,0:T(8,128)(2,1)S(1)}, u32[]{:S(2)}, u32[]{:S(2)}) collective-permute-start(bf16[16,4096]{1,0:T(8,128)(2,1)} %refs_2_.1), channel_id=1, source_target_pairs={{0,8},{4,12},{8,0},{12,4},{16,24},{20,28},{24,16},{28,20},{1,9},{5... | collective-permute-start | bytes 393224 | tf_op jit(solution)/shard_map/ppermute | solution.py:20
  3.7 1.5 %collective-permute-start.2 = (bf16[16,4096]{1,0:T(8,128)(2,1)}, bf16[16,4096]{1,0:T(8,128)(2,1)S(1)}, u32[]{:S(2)}, u32[]{:S(2)}) collective-permute-start(bf16[16,4096]{1,0:T(8,128)(2,1)} %refs_2_.1), channel_id=1, source_target_pairs={{0,16},{4,20},{8,24},{12,28},{16,0},{20,4},{24,8},{28,12},{1,17},{... | collective-permute-start | bytes 393224 | tf_op jit(solution)/shard_map/ppermute | solution.py:20
  5.2 2.7 %collective-permute-done.refs_0_ = bf16[16,4096]{1,0:T(8,128)(2,1)S(1)} collective-permute-done((bf16[16,4096]{1,0:T(8,128)(2,1)}, bf16[16,4096]{1,0:T(8,128)(2,1)S(1)}, u32[]{:S(2)}, u32[]{:S(2)}) %collective-permute-start) | collective-permute-done | bytes 131104 | tf_op jit(solution)/shard_map/ppermute | solution.py:20
  7.9 3.8 %collective-permute-done.2.refs_1_ = bf16[16,4096]{1,0:T(8,128)(2,1)S(1)} collective-permute-done((bf16[16,4096]{1,0:T(8,128)(2,1)}, bf16[16,4096]{1,0:T(8,128)(2,1)S(1)}, u32[]{:S(2)}, u32[]{:S(2)}) %collective-permute-start.2) | collective-permute-done | bytes 131104 | tf_op jit(solution)/shard_map/ppermute | solution.py:20
  12.2 4.5 %prepare.1 = (bf16[512,4096]{1,0:T(8,128)(2,1)S(1)}, bf16[512,4096]{1,0:T(8,128)(2,1)S(1)}, f32[128,128]{1,0:T(8,128)S(1)}) custom-call(bf16[512,4096]{1,0:T(8,128)(2,1)} %particles.1, bf16[512,4096]{1,0:T(8,128)(2,1)} %ctf.1, f32[1,4096]{1,0:T(1,128)} %bitcast.5, s32[1,128]{1,0:T(1,128)} %bitcast.6, f32[1,5]{1,0:T(1,128)} %bitcast.7), custom_call_target="tpu_custom_call" | custom-call | flops 33554432 | bytes 16777216 | tf_op jit(solution)/shard_map/prepare/pallas_call | solution.py:85
  16.9 1.3 %score.1 = (f32[128,128]{1,0:T(8,128)S(1)}, f32[128,128]{1,0:T(8,128)S(1)}, bf16[128,4096]{1,0:T(8,128)(2,1)S(1)}, bf16[128,4096]{1,0:T(8,128)(2,1)S(1)}) custom-call(bf16[16,4096]{1,0:T(8,128)(2,1)S(1)} %collective-permute-done.1.refs_0_, bf16[16,4096]{1,0:T(8,128)(2,1)S(1)} %collective-permute-done.3.refs_1_, ...), custom_call_target="tpu_custom_call" | custom-call | flops 1073741824 | bytes 8388608 | tf_op jit(solution)/shard_map/score/pallas_call | solution.py:163
  18.3 0.8 %own_score.3 = f32[128,128]{1,0:T(8,128)S(1)} custom-call(bf16[128,4096]{1,0:T(8,128)(2,1)S(1)} %get-tuple-element.23.lines, bf16[128,4096]{1,0:T(8,128)(2,1)S(1)} %get-tuple-element.24.square, bf16[512,4096]{1,0:T(8,128)(2,1)S(1)} %get-tuple-element.21.refs_6_.weighted.refs_4_, bf16[512,4096]{1,0:T(8,128)(2,1)S(1)} %get-tuple-element.22.refs_7_.quadratic), custom_call_target="tpu_custom_call" | custom-call | flops 268435456 | bytes 2097152 | tf_op jit(solution)/shard_map/own_score/pallas_call | solution.py:187
  19.0 1.6 %collective-permute-start.9 = (f32[128,128]{1,0:T(8,128)S(1)}, f32[128,128]{1,0:T(8,128)S(1)}, u32[]{:S(2)}, u32[]{:S(2)}) collective-permute-start(f32[128,128]{1,0:T(8,128)S(1)} %own_score.3), channel_id=1, source_target_pairs={{0,1},{1,0},{2,3},{3,2},{4,5},{5,4},{6,7},{7,6},{8,9},{9,8},{10,11... | collective-permute-start | bytes 196616 | tf_op jit(solution)/shard_map/ppermute | solution.py:20
  20.7 2.6 %collective-permute-start.7 = (f32[128,128]{1,0:T(8,128)S(1)}, f32[128,128]{1,0:T(8,128)S(1)}, u32[]{:S(2)}, u32[]{:S(2)}) collective-permute-start(f32[128,128]{1,0:T(8,128)S(1)} %get-tuple-element.25), channel_id=1, source_target_pairs={{0,2},{1,3},{2,0},{3,1},{4,6},{5,7},{6,4},{7,5},{8,10},{9,11},{10,... | collective-permute-start | bytes 196616 | tf_op jit(solution)/shard_map/ppermute | solution.py:20
  24.2 0.8 %own_score.2.refs_0_ = f32[128,128]{1,0:T(8,128)S(1)} custom-call(bf16[128,4096]{1,0:T(8,128)(2,1)S(1)} %get-tuple-element.23.lines, bf16[128,4096]{1,0:T(8,128)(2,1)S(1)} %get-tuple-element.24.square, bf16[512,4096]{1,0:T(8,128)(2,1)S(1)} %get-tuple-element.21.refs_6_.weighted.refs_4_, bf16[512,4096]{1,0:T(8,128)(2,1)S(1)} %get-tuple-element.22.refs_7_.quadratic), custom_call_target="tpu_custom_call" | custom-call | flops 268435456 | bytes 2097152 | tf_op jit(solution)/shard_map/own_score/pallas_call | solution.py:187
  24.9 3.2 %collective-permute-done.7.refs_1_ = f32[128,128]{1,0:T(8,128)S(1)} collective-permute-done((f32[128,128]{1,0:T(8,128)S(1)}, f32[128,128]{1,0:T(8,128)S(1)}, u32[]{:S(2)}, u32[]{:S(2)}) %collective-permute-start.7) | collective-permute-done | bytes 65568 | tf_op jit(solution)/shard_map/ppermute | solution.py:20
  28.1 1.3 %collective-permute-done.8.refs_2_ = f32[128,128]{1,0:T(8,128)S(1)} collective-permute-done((f32[128,128]{1,0:T(8,128)S(1)}, f32[128,128]{1,0:T(8,128)S(1)}, u32[]{:S(2)}, u32[]{:S(2)}) %collective-permute-start.8) | collective-permute-done | bytes 65568 | tf_op jit(solution)/shard_map/ppermute | solution.py:20
  29.5 0.8 %collective-permute-start.10 = (bf16[144,128]{1,0:T(8,128)(2,1)S(1)}, bf16[144,128]{1,0:T(8,128)(2,1)S(1)}, u32[]{:S(2)}, u32[]{:S(2)}) collective-permute-start(bf16[144,128]{1,0:T(8,128)(2,1)S(1)} %weigh.1.refs_0_), channel_id=1, source_target_pairs={{0,1},{1,0},{2,3},{3,2},{4,5},{5,4},{6,7},{7,6},{8,9},{9,8},{10,11... | collective-permute-start | bytes 110600 | tf_op jit(solution)/shard_map/ppermute | solution.py:20
  30.3 1.7 %collective-permute-start.11 = (bf16[144,128]{1,0:T(8,128)(2,1)S(1)}, bf16[144,128]{1,0:T(8,128)(2,1)S(1)}, u32[]{:S(2)}, u32[]{:S(2)}) collective-permute-start(bf16[144,128]{1,0:T(8,128)(2,1)S(1)} %weigh.1.refs_0_), channel_id=1, source_target_pairs={{0,2},{1,3},{2,0},{3,1},{4,6},{5,7},{6,4},{7,5},{8,10},{9,11},{10,... | collective-permute-start | bytes 110600 | tf_op jit(solution)/shard_map/ppermute | solution.py:20
  32.0 2.0 %collective-permute-start.12 = (bf16[144,128]{1,0:T(8,128)(2,1)S(1)}, bf16[144,128]{1,0:T(8,128)(2,1)S(1)}, u32[]{:S(2)}, u32[]{:S(2)}) collective-permute-start(bf16[144,128]{1,0:T(8,128)(2,1)S(1)} %weigh.1.refs_0_), channel_id=1, source_target_pairs={{0,3},{1,2},{2,1},{3,0},{4,7},{5,6},{6,5},{7,4},{8,11},{9,10},{10,... | collective-permute-start | bytes 110600 | tf_op jit(solution)/shard_map/ppermute | solution.py:20
  34.0 1.2 %collective-permute-done.11.refs_2_ = bf16[144,128]{1,0:T(8,128)(2,1)S(1)} collective-permute-done((bf16[144,128]{1,0:T(8,128)(2,1)S(1)}, bf16[144,128]{1,0:T(8,128)(2,1)S(1)}, u32[]{:S(2)}, u32[]{:S(2)}) %collective-permute-start.11) | collective-permute-done | bytes 36896 | tf_op jit(solution)/shard_map/ppermute | solution.py:20
  35.2 2.6 %collective-permute-done.12.refs_3_ = bf16[144,128]{1,0:T(8,128)(2,1)S(1)} collective-permute-done((bf16[144,128]{1,0:T(8,128)(2,1)S(1)}, bf16[144,128]{1,0:T(8,128)(2,1)S(1)}, u32[]{:S(2)}, u32[]{:S(2)}) %collective-permute-start.12) | collective-permute-done | bytes 36896 | tf_op jit(solution)/shard_map/ppermute | solution.py:20
  39.1 1.0 %collective-permute-done.14.got = bf16[32,4096]{1,0:T(8,128)(2,1)S(1)} collective-permute-done((bf16[32,4096]{1,0:T(8,128)(2,1)S(1)}, bf16[32,4096]{1,0:T(8,128)(2,1)S(1)}, u32[]{:S(2)}, u32[]{:S(2)}) %collective-permute-start.14) | collective-permute-done | bytes 262176 | tf_op jit(solution)/shard_map/ppermute | solution.py:20
  40.2 1.3 %collective-permute-start.15 = (bf16[16,4096]{1,0:T(8,128)(2,1)S(1)}, bf16[16,4096]{1,0:T(8,128)(2,1)S(1)}, u32[]{:S(2)}, u32[]{:S(2)}) collective-permute-start(bf16[16,4096]{1,0:T(8,128)(2,1)S(1)} %get-tuple-element.32), channel_id=1, source_target_pairs={{0,8},{4,12},{8,0},{12,4},{16,24},{20,28},{24,16},{28,20},{1,9},{5... | collective-permute-start | bytes 393224 | tf_op jit(solution)/shard_map/ppermute | solution.py:20
  41.4 0.8 %collective-permute-start.16 = (bf16[16,4096]{1,0:T(8,128)(2,1)S(1)}, bf16[16,4096]{1,0:T(8,128)(2,1)S(1)}, u32[]{:S(2)}, u32[]{:S(2)}) collective-permute-start(bf16[16,4096]{1,0:T(8,128)(2,1)S(1)} %get-tuple-element.33), channel_id=1, source_target_pairs={{0,16},{4,20},{8,24},{12,28},{16,0},{20,4},{24,8},{28,12},{1,17},{... | collective-permute-start | bytes 393224 | tf_op jit(solution)/shard_map/ppermute | solution.py:20
  42.3 1.5 %collective-permute-start.17 = (bf16[16,4096]{1,0:T(8,128)(2,1)S(1)}, bf16[16,4096]{1,0:T(8,128)(2,1)S(1)}, u32[]{:S(2)}, u32[]{:S(2)}) collective-permute-start(bf16[16,4096]{1,0:T(8,128)(2,1)S(1)} %get-tuple-element.34), channel_id=1, source_target_pairs={{0,24},{4,28},{8,16},{12,20},{16,8},{20,12},{24,0},{28,4},{1,25},{... | collective-permute-start | bytes 393224 | tf_op jit(solution)/shard_map/ppermute | solution.py:20
  44.4 1.9 %collective-permute-done.15.refs_0_ = bf16[16,4096]{1,0:T(8,128)(2,1)S(1)} collective-permute-done((bf16[16,4096]{1,0:T(8,128)(2,1)S(1)}, bf16[16,4096]{1,0:T(8,128)(2,1)S(1)}, u32[]{:S(2)}, u32[]{:S(2)}) %collective-permute-start.15) | collective-permute-done | bytes 131104 | tf_op jit(solution)/shard_map/ppermute | solution.py:20
  46.3 1.6 %collective-permute-done.16.refs_1_ = bf16[16,4096]{1,0:T(8,128)(2,1)S(1)} collective-permute-done((bf16[16,4096]{1,0:T(8,128)(2,1)S(1)}, bf16[16,4096]{1,0:T(8,128)(2,1)S(1)}, u32[]{:S(2)}, u32[]{:S(2)}) %collective-permute-start.16) | collective-permute-done | bytes 131104 | tf_op jit(solution)/shard_map/ppermute | solution.py:20
  47.9 1.6 %collective-permute-done.17.refs_2_ = bf16[16,4096]{1,0:T(8,128)(2,1)S(1)} collective-permute-done((bf16[16,4096]{1,0:T(8,128)(2,1)S(1)}, bf16[16,4096]{1,0:T(8,128)(2,1)S(1)}, u32[]{:S(2)}, u32[]{:S(2)}) %collective-permute-start.17) | collective-permute-done | bytes 131104 | tf_op jit(solution)/shard_map/ppermute | solution.py:20
  (25 shorter events, 3.7 us)
Async XLA Ops:
  0.6 7.2 %collective-permute-start = (bf16[16,4096]{1,0:T(8,128)(2,1)}, bf16[16,4096]{1,0:T(8,128)(2,1)S(1)}, u32[]{:S(2)}, u32[]{:S(2)}) collective-permute-start(bf16[16,4096]{1,0:T(8,128)(2,1)} %refs_2_.1), channel_id=1, source_target_pairs={{0,8},{4,12},{8,0},{12,4},{16,24},{20,28},{24,16},{28,20},{1,9},{5... | collective-permute-start | bytes 393224 | tf_op jit(solution)/shard_map/ppermute | solution.py:20
  3.7 8.0 %collective-permute-start.2 = (bf16[16,4096]{1,0:T(8,128)(2,1)}, bf16[16,4096]{1,0:T(8,128)(2,1)S(1)}, u32[]{:S(2)}, u32[]{:S(2)}) collective-permute-start(bf16[16,4096]{1,0:T(8,128)(2,1)} %refs_2_.1), channel_id=1, source_target_pairs={{0,16},{4,20},{8,24},{12,28},{16,0},{20,4},{24,8},{28,12},{1,17},{... | collective-permute-start | bytes 393224 | tf_op jit(solution)/shard_map/ppermute | solution.py:20
  5.2 6.5 %collective-permute-start.5 = (bf16[16,4096]{1,0:T(8,128)(2,1)}, bf16[16,4096]{1,0:T(8,128)(2,1)S(1)}, u32[]{:S(2)}, u32[]{:S(2)}) collective-permute-start(bf16[16,4096]{1,0:T(8,128)(2,1)} %refs_2_.1), channel_id=1, source_target_pairs={{0,24},{4,28},{8,16},{12,20},{16,8},{20,12},{24,0},{28,4},{1,25},{... | collective-permute-start | bytes 393224 | tf_op jit(solution)/shard_map/ppermute | solution.py:20
  5.2 11.7 %collective-permute-start.4 = (bf16[16,4096]{1,0:T(8,128)(2,1)}, bf16[16,4096]{1,0:T(8,128)(2,1)S(1)}, u32[]{:S(2)}, u32[]{:S(2)}) collective-permute-start(bf16[16,4096]{1,0:T(8,128)(2,1)} %refs_2_.1), channel_id=1, source_target_pairs={{0,4},{4,0},{8,12},{12,8},{16,20},{20,16},{24,28},{28,24},{1,5},{5... | collective-permute-start | bytes 393224 | tf_op jit(solution)/shard_map/ppermute | solution.py:20
  7.9 9.1 %collective-permute-start.1 = (bf16[16,4096]{1,0:T(8,128)(2,1)S(1)}, bf16[16,4096]{1,0:T(8,128)(2,1)S(1)}, u32[]{:S(2)}, u32[]{:S(2)}) collective-permute-start(bf16[16,4096]{1,0:T(8,128)(2,1)S(1)} %collective-permute-done.refs_0_), channel_id=1, source_target_pairs={{0,4},{4,0},{8,12},{12,8},{16,20},{20,16},{24,28},{28,24},{1,5},{5... | collective-permute-start | bytes 393224 | tf_op jit(solution)/shard_map/ppermute | solution.py:20
  11.7 5.3 %collective-permute-start.3 = (bf16[16,4096]{1,0:T(8,128)(2,1)S(1)}, bf16[16,4096]{1,0:T(8,128)(2,1)S(1)}, u32[]{:S(2)}, u32[]{:S(2)}) collective-permute-start(bf16[16,4096]{1,0:T(8,128)(2,1)S(1)} %collective-permute-done.2.refs_1_), channel_id=1, source_target_pairs={{0,4},{4,0},{8,12},{12,8},{16,20},{20,16},{24,28},{28,24},{1,5},{5... | collective-permute-start | bytes 393224 | tf_op jit(solution)/shard_map/ppermute | solution.py:20
  11.7 5.3 %collective-permute-start.6 = (bf16[16,4096]{1,0:T(8,128)(2,1)S(1)}, bf16[16,4096]{1,0:T(8,128)(2,1)S(1)}, u32[]{:S(2)}, u32[]{:S(2)}) collective-permute-start(bf16[16,4096]{1,0:T(8,128)(2,1)S(1)} %collective-permute-done.5.refs_3_), channel_id=1, source_target_pairs={{0,4},{4,0},{8,12},{12,8},{16,20},{20,16},{24,28},{28,24},{1,5},{5... | collective-permute-start | bytes 393224 | tf_op jit(solution)/shard_map/ppermute | solution.py:20
  12.2 4.6 %copy-start = (bf16[16,4096]{1,0:T(8,128)(2,1)S(1)}, bf16[16,4096]{1,0:T(8,128)(2,1)}, u32[]{:S(2)}) copy-start(bf16[16,4096]{1,0:T(8,128)(2,1)} %refs_2_.1) | copy-start | bytes 393220
  19.0 5.9 %collective-permute-start.9 = (f32[128,128]{1,0:T(8,128)S(1)}, f32[128,128]{1,0:T(8,128)S(1)}, u32[]{:S(2)}, u32[]{:S(2)}) collective-permute-start(f32[128,128]{1,0:T(8,128)S(1)} %own_score.3), channel_id=1, source_target_pairs={{0,1},{1,0},{2,3},{3,2},{4,5},{5,4},{6,7},{7,6},{8,9},{9,8},{10,11... | collective-permute-start | bytes 196616 | tf_op jit(solution)/shard_map/ppermute | solution.py:20
  20.7 7.5 %collective-permute-start.7 = (f32[128,128]{1,0:T(8,128)S(1)}, f32[128,128]{1,0:T(8,128)S(1)}, u32[]{:S(2)}, u32[]{:S(2)}) collective-permute-start(f32[128,128]{1,0:T(8,128)S(1)} %get-tuple-element.25), channel_id=1, source_target_pairs={{0,2},{1,3},{2,0},{3,1},{4,6},{5,7},{6,4},{7,5},{8,10},{9,11},{10,... | collective-permute-start | bytes 196616 | tf_op jit(solution)/shard_map/ppermute | solution.py:20
  23.3 6.2 %collective-permute-start.8 = (f32[128,128]{1,0:T(8,128)S(1)}, f32[128,128]{1,0:T(8,128)S(1)}, u32[]{:S(2)}, u32[]{:S(2)}) collective-permute-start(f32[128,128]{1,0:T(8,128)S(1)} %get-tuple-element.26), channel_id=1, source_target_pairs={{0,3},{1,2},{2,1},{3,0},{4,7},{5,6},{6,5},{7,4},{8,11},{9,10},{10,... | collective-permute-start | bytes 196616 | tf_op jit(solution)/shard_map/ppermute | solution.py:20
  29.5 4.5 %collective-permute-start.10 = (bf16[144,128]{1,0:T(8,128)(2,1)S(1)}, bf16[144,128]{1,0:T(8,128)(2,1)S(1)}, u32[]{:S(2)}, u32[]{:S(2)}) collective-permute-start(bf16[144,128]{1,0:T(8,128)(2,1)S(1)} %weigh.1.refs_0_), channel_id=1, source_target_pairs={{0,1},{1,0},{2,3},{3,2},{4,5},{5,4},{6,7},{7,6},{8,9},{9,8},{10,11... | collective-permute-start | bytes 110600 | tf_op jit(solution)/shard_map/ppermute | solution.py:20
  30.3 4.9 %collective-permute-start.11 = (bf16[144,128]{1,0:T(8,128)(2,1)S(1)}, bf16[144,128]{1,0:T(8,128)(2,1)S(1)}, u32[]{:S(2)}, u32[]{:S(2)}) collective-permute-start(bf16[144,128]{1,0:T(8,128)(2,1)S(1)} %weigh.1.refs_0_), channel_id=1, source_target_pairs={{0,2},{1,3},{2,0},{3,1},{4,6},{5,7},{6,4},{7,5},{8,10},{9,11},{10,... | collective-permute-start | bytes 110600 | tf_op jit(solution)/shard_map/ppermute | solution.py:20
  32.0 5.8 %collective-permute-start.12 = (bf16[144,128]{1,0:T(8,128)(2,1)S(1)}, bf16[144,128]{1,0:T(8,128)(2,1)S(1)}, u32[]{:S(2)}, u32[]{:S(2)}) collective-permute-start(bf16[144,128]{1,0:T(8,128)(2,1)S(1)} %weigh.1.refs_0_), channel_id=1, source_target_pairs={{0,3},{1,2},{2,1},{3,0},{4,7},{5,6},{6,5},{7,4},{8,11},{9,10},{10,... | collective-permute-start | bytes 110600 | tf_op jit(solution)/shard_map/ppermute | solution.py:20
  38.5 1.6 %collective-permute-start.14 = (bf16[32,4096]{1,0:T(8,128)(2,1)S(1)}, bf16[32,4096]{1,0:T(8,128)(2,1)S(1)}, u32[]{:S(2)}, u32[]{:S(2)}) collective-permute-start(bf16[32,4096]{1,0:T(8,128)(2,1)S(1)} %get-tuple-element.31), channel_id=1, source_target_pairs={{0,4},{4,0},{8,12},{12,8},{16,20},{20,16},{24,28},{28,24},{1,5},{5... | collective-permute-start | bytes 786440 | tf_op jit(solution)/shard_map/ppermute | solution.py:20
  38.6 3.7 %collective-permute-start.13 = (bf16[32,4096]{1,0:T(8,128)(2,1)S(1)}, bf16[32,4096]{1,0:T(8,128)(2,1)S(1)}, u32[]{:S(2)}, u32[]{:S(2)}) collective-permute-start(bf16[32,4096]{1,0:T(8,128)(2,1)S(1)} %get-tuple-element.29), channel_id=1, source_target_pairs={{0,4},{4,0},{8,12},{12,8},{16,20},{20,16},{24,28},{28,24},{1,5},{5... | collective-permute-start | bytes 786440 | tf_op jit(solution)/shard_map/ppermute | solution.py:20
  40.2 6.2 %collective-permute-start.15 = (bf16[16,4096]{1,0:T(8,128)(2,1)S(1)}, bf16[16,4096]{1,0:T(8,128)(2,1)S(1)}, u32[]{:S(2)}, u32[]{:S(2)}) collective-permute-start(bf16[16,4096]{1,0:T(8,128)(2,1)S(1)} %get-tuple-element.32), channel_id=1, source_target_pairs={{0,8},{4,12},{8,0},{12,4},{16,24},{20,28},{24,16},{28,20},{1,9},{5... | collective-permute-start | bytes 393224 | tf_op jit(solution)/shard_map/ppermute | solution.py:20
  41.4 6.5 %collective-permute-start.16 = (bf16[16,4096]{1,0:T(8,128)(2,1)S(1)}, bf16[16,4096]{1,0:T(8,128)(2,1)S(1)}, u32[]{:S(2)}, u32[]{:S(2)}) collective-permute-start(bf16[16,4096]{1,0:T(8,128)(2,1)S(1)} %get-tuple-element.33), channel_id=1, source_target_pairs={{0,16},{4,20},{8,24},{12,28},{16,0},{20,4},{24,8},{28,12},{1,17},{... | collective-permute-start | bytes 393224 | tf_op jit(solution)/shard_map/ppermute | solution.py:20
  42.3 7.2 %collective-permute-start.17 = (bf16[16,4096]{1,0:T(8,128)(2,1)S(1)}, bf16[16,4096]{1,0:T(8,128)(2,1)S(1)}, u32[]{:S(2)}, u32[]{:S(2)}) collective-permute-start(bf16[16,4096]{1,0:T(8,128)(2,1)S(1)} %get-tuple-element.34), channel_id=1, source_target_pairs={{0,24},{4,28},{8,16},{12,20},{16,8},{20,12},{24,0},{28,4},{1,25},{... | collective-permute-start | bytes 393224 | tf_op jit(solution)/shard_map/ppermute | solution.py:20

commit v5 on v4

--- a/solution.py
+++ b/solution.py
@@ -331,7 +331,7 @@
 def body(blk, pix, particles, ctf, noise_var, projections, orient_class, class_prior, counts):
     rows = projections.shape[0]
     even = list(range(2, blk, 2))
-    lead = even[:-1] + [0] + even[-1:]
+    lead = even[:1] + [0] + even[1:]
     order = lead + [k ^ 1 for k in lead]
     noise, orient_class, class_prior = (value.reshape(1, -1) for value in (noise_var, orient_class, class_prior))
     far = {0: projections}
@@ -354,14 +354,14 @@
     parts = [weights]
     for j in range(1, pix):
         parts.append(swap(weights, "pix", pix, j))
-    first = rows * (len(lead) - 2)
+    first = rows
     kept, sent, late, norm = field(parts, weighted, first)
     sent = swap(sent, "blk", blk, 1)
     late = swap(late, "blk", blk, 1)
-    out = list(pair(kept, sent, rows, 0, [BF16] * (len(lead) - 2)))
-    own, last = pair(kept, late, rows, first, [F32, BF16])
+    out = list(pair(kept, sent, rows, 0, [BF16]))
+    own, *last = pair(kept, late, rows, first, [F32] + [BF16] * (len(lead) - 2))
     got = []
-    for piece, k in zip(out + [last], even):
+    for piece, k in zip(out + last, even):
         got.append(swap(piece, "blk", blk, k))
     return final(own, got), norm.reshape(-1)
 

time: 50.4 us -> 50.9 us (level)
  transfers between devices with their start and end apart: 18 -> 18, of which waited for: 10 -> 9; matrix products, arithmetic and copies ran while one was open for 1% -> 1% of each run, Pallas kernels for 11% -> 11%
where the time goes in v5:
time: 50.9 us; the launch traced here: 50.8 us
  waiting for transfers between devices  21.4 us (42%)
  starting transfers between devices  18.2 us (36%)
  Pallas kernels  9.22 us (18%)
  between operations  1.4 us (3%)
  local copies, waits for them, and re-layouts  0.58 us (1%)
    ppermute x18, waiting for transfers between devices, swap(): out = lax.ppermute(value, axis, [(i, i ^ k) for i in range(size)])  21.4 us
    ppermute x18, starting transfers between devices, swap(): out = lax.ppermute(value, axis, [(i, i ^ k) for i in range(size)])  18.2 us
    pallas_call x1, Pallas kernels, prepare(): pl.pallas_call(functools.partial(prepare_kernel, order, rows), out_shape=...  4.55 us
    pallas_call x2, Pallas kernels, own_score(): pl.pallas_call(functools.partial(own_kernel, base), out_shape=pltpu.VMEM(...  1.54 us
    pallas_call x1, Pallas kernels, score(): pl.pallas_call(functools.partial(score_kernel, len(proj)), out_shape=tupl...  1.32 us
  transfers between devices with their start and end apart: 18, of which 9 were waited for; matrix products, arithmetic and copies ran while one was open for 1% of the time, Pallas kernels for 11%

profile of v5, /device:TPU:0, one launch (start us, length us, event | category | flops | bytes accessed | tf_op | source)
XLA Modules:
  0.0 50.8 jit_solution(12675248316512198484)
XLA Ops:
  0.6 3.0 %collective-permute-start = (bf16[16,4096]{1,0:T(8,128)(2,1)}, bf16[16,4096]{1,0:T(8,128)(2,1)S(1)}, u32[]{:S(2)}, u32[]{:S(2)}) collective-permute-start(bf16[16,4096]{1,0:T(8,128)(2,1)} %refs_1_.1), channel_id=1, source_target_pairs={{0,8},{4,12},{8,0},{12,4},{16,24},{20,28},{24,16},{28,20},{1,9},{5... | collective-permute-start | bytes 393224 | tf_op jit(solution)/shard_map/ppermute | solution.py:20
  3.7 1.5 %collective-permute-start.3 = (bf16[16,4096]{1,0:T(8,128)(2,1)}, bf16[16,4096]{1,0:T(8,128)(2,1)S(1)}, u32[]{:S(2)}, u32[]{:S(2)}) collective-permute-start(bf16[16,4096]{1,0:T(8,128)(2,1)} %refs_1_.1), channel_id=1, source_target_pairs={{0,16},{4,20},{8,24},{12,28},{16,0},{20,4},{24,8},{28,12},{1,17},{... | collective-permute-start | bytes 393224 | tf_op jit(solution)/shard_map/ppermute | solution.py:20
  5.2 2.7 %collective-permute-done.refs_0_ = bf16[16,4096]{1,0:T(8,128)(2,1)S(1)} collective-permute-done((bf16[16,4096]{1,0:T(8,128)(2,1)}, bf16[16,4096]{1,0:T(8,128)(2,1)S(1)}, u32[]{:S(2)}, u32[]{:S(2)}) %collective-permute-start) | collective-permute-done | bytes 131104 | tf_op jit(solution)/shard_map/ppermute | solution.py:20
  7.9 3.8 %collective-permute-done.3.refs_2_ = bf16[16,4096]{1,0:T(8,128)(2,1)S(1)} collective-permute-done((bf16[16,4096]{1,0:T(8,128)(2,1)}, bf16[16,4096]{1,0:T(8,128)(2,1)S(1)}, u32[]{:S(2)}, u32[]{:S(2)}) %collective-permute-start.3) | collective-permute-done | bytes 131104 | tf_op jit(solution)/shard_map/ppermute | solution.py:20
  12.2 4.5 %prepare.1 = (bf16[512,4096]{1,0:T(8,128)(2,1)S(1)}, bf16[512,4096]{1,0:T(8,128)(2,1)S(1)}, f32[128,128]{1,0:T(8,128)S(1)}) custom-call(bf16[512,4096]{1,0:T(8,128)(2,1)} %particles.1, bf16[512,4096]{1,0:T(8,128)(2,1)} %ctf.1, f32[1,4096]{1,0:T(1,128)} %bitcast.5, s32[1,128]{1,0:T(1,128)} %bitcast.6, f32[1,5]{1,0:T(1,128)} %bitcast.7), custom_call_target="tpu_custom_call" | custom-call | flops 33554432 | bytes 16777216 | tf_op jit(solution)/shard_map/prepare/pallas_call | solution.py:85
  16.9 1.3 %score.1 = (f32[128,128]{1,0:T(8,128)S(1)}, f32[128,128]{1,0:T(8,128)S(1)}, bf16[128,4096]{1,0:T(8,128)(2,1)S(1)}, bf16[128,4096]{1,0:T(8,128)(2,1)S(1)}) custom-call(bf16[16,4096]{1,0:T(8,128)(2,1)S(1)} %collective-permute-done.1.refs_0_, bf16[16,4096]{1,0:T(8,128)(2,1)S(1)} %collective-permute-done.2.refs_1_, ...), custom_call_target="tpu_custom_call" | custom-call | flops 1073741824 | bytes 8388608 | tf_op jit(solution)/shard_map/score/pallas_call | solution.py:163
  18.3 0.8 %own_score.3 = f32[128,128]{1,0:T(8,128)S(1)} custom-call(bf16[128,4096]{1,0:T(8,128)(2,1)S(1)} %get-tuple-element.22.lines, bf16[128,4096]{1,0:T(8,128)(2,1)S(1)} %get-tuple-element.23.square, bf16[512,4096]{1,0:T(8,128)(2,1)S(1)} %get-tuple-element.20.refs_6_.weighted.refs_4_, bf16[512,4096]{1,0:T(8,128)(2,1)S(1)} %get-tuple-element.21.refs_7_.quadratic), custom_call_target="tpu_custom_call" | custom-call | flops 268435456 | bytes 2097152 | tf_op jit(solution)/shard_map/own_score/pallas_call | solution.py:187
  19.0 1.6 %collective-permute-start.9 = (f32[128,128]{1,0:T(8,128)S(1)}, f32[128,128]{1,0:T(8,128)S(1)}, u32[]{:S(2)}, u32[]{:S(2)}) collective-permute-start(f32[128,128]{1,0:T(8,128)S(1)} %own_score.3), channel_id=1, source_target_pairs={{0,1},{1,0},{2,3},{3,2},{4,5},{5,4},{6,7},{7,6},{8,9},{9,8},{10,11... | collective-permute-start | bytes 196616 | tf_op jit(solution)/shard_map/ppermute | solution.py:20
  20.7 2.6 %collective-permute-start.7 = (f32[128,128]{1,0:T(8,128)S(1)}, f32[128,128]{1,0:T(8,128)S(1)}, u32[]{:S(2)}, u32[]{:S(2)}) collective-permute-start(f32[128,128]{1,0:T(8,128)S(1)} %get-tuple-element.24), channel_id=1, source_target_pairs={{0,2},{1,3},{2,0},{3,1},{4,6},{5,7},{6,4},{7,5},{8,10},{9,11},{10,... | collective-permute-start | bytes 196616 | tf_op jit(solution)/shard_map/ppermute | solution.py:20
  24.2 0.8 %own_score.2.refs_0_ = f32[128,128]{1,0:T(8,128)S(1)} custom-call(bf16[128,4096]{1,0:T(8,128)(2,1)S(1)} %get-tuple-element.22.lines, bf16[128,4096]{1,0:T(8,128)(2,1)S(1)} %get-tuple-element.23.square, bf16[512,4096]{1,0:T(8,128)(2,1)S(1)} %get-tuple-element.20.refs_6_.weighted.refs_4_, bf16[512,4096]{1,0:T(8,128)(2,1)S(1)} %get-tuple-element.21.refs_7_.quadratic), custom_call_target="tpu_custom_call" | custom-call | flops 268435456 | bytes 2097152 | tf_op jit(solution)/shard_map/own_score/pallas_call | solution.py:187
  24.9 3.2 %collective-permute-done.7.refs_1_ = f32[128,128]{1,0:T(8,128)S(1)} collective-permute-done((f32[128,128]{1,0:T(8,128)S(1)}, f32[128,128]{1,0:T(8,128)S(1)}, u32[]{:S(2)}, u32[]{:S(2)}) %collective-permute-start.7) | collective-permute-done | bytes 65568 | tf_op jit(solution)/shard_map/ppermute | solution.py:20
  28.1 1.3 %collective-permute-done.8.refs_2_ = f32[128,128]{1,0:T(8,128)S(1)} collective-permute-done((f32[128,128]{1,0:T(8,128)S(1)}, f32[128,128]{1,0:T(8,128)S(1)}, u32[]{:S(2)}, u32[]{:S(2)}) %collective-permute-start.8) | collective-permute-done | bytes 65568 | tf_op jit(solution)/shard_map/ppermute | solution.py:20
  29.5 0.8 %collective-permute-start.10 = (bf16[144,128]{1,0:T(8,128)(2,1)S(1)}, bf16[144,128]{1,0:T(8,128)(2,1)S(1)}, u32[]{:S(2)}, u32[]{:S(2)}) collective-permute-start(bf16[144,128]{1,0:T(8,128)(2,1)S(1)} %weigh.1.refs_0_), channel_id=1, source_target_pairs={{0,1},{1,0},{2,3},{3,2},{4,5},{5,4},{6,7},{7,6},{8,9},{9,8},{10,11... | collective-permute-start | bytes 110600 | tf_op jit(solution)/shard_map/ppermute | solution.py:20
  30.3 1.7 %collective-permute-start.11 = (bf16[144,128]{1,0:T(8,128)(2,1)S(1)}, bf16[144,128]{1,0:T(8,128)(2,1)S(1)}, u32[]{:S(2)}, u32[]{:S(2)}) collective-permute-start(bf16[144,128]{1,0:T(8,128)(2,1)S(1)} %weigh.1.refs_0_), channel_id=1, source_target_pairs={{0,2},{1,3},{2,0},{3,1},{4,6},{5,7},{6,4},{7,5},{8,10},{9,11},{10,... | collective-permute-start | bytes 110600 | tf_op jit(solution)/shard_map/ppermute | solution.py:20
  32.0 2.0 %collective-permute-start.12 = (bf16[144,128]{1,0:T(8,128)(2,1)S(1)}, bf16[144,128]{1,0:T(8,128)(2,1)S(1)}, u32[]{:S(2)}, u32[]{:S(2)}) collective-permute-start(bf16[144,128]{1,0:T(8,128)(2,1)S(1)} %weigh.1.refs_0_), channel_id=1, source_target_pairs={{0,3},{1,2},{2,1},{3,0},{4,7},{5,6},{6,5},{7,4},{8,11},{9,10},{10,... | collective-permute-start | bytes 110600 | tf_op jit(solution)/shard_map/ppermute | solution.py:20
  34.0 1.2 %collective-permute-done.11.refs_2_ = bf16[144,128]{1,0:T(8,128)(2,1)S(1)} collective-permute-done((bf16[144,128]{1,0:T(8,128)(2,1)S(1)}, bf16[144,128]{1,0:T(8,128)(2,1)S(1)}, u32[]{:S(2)}, u32[]{:S(2)}) %collective-permute-start.11) | collective-permute-done | bytes 36896 | tf_op jit(solution)/shard_map/ppermute | solution.py:20
  35.2 2.6 %collective-permute-done.12.refs_3_ = bf16[144,128]{1,0:T(8,128)(2,1)S(1)} collective-permute-done((bf16[144,128]{1,0:T(8,128)(2,1)S(1)}, bf16[144,128]{1,0:T(8,128)(2,1)S(1)}, u32[]{:S(2)}, u32[]{:S(2)}) %collective-permute-start.12) | collective-permute-done | bytes 36896 | tf_op jit(solution)/shard_map/ppermute | solution.py:20
  39.1 1.4 %collective-permute-done.14.got = bf16[16,4096]{1,0:T(8,128)(2,1)S(1)} collective-permute-done((bf16[16,4096]{1,0:T(8,128)(2,1)S(1)}, bf16[16,4096]{1,0:T(8,128)(2,1)S(1)}, u32[]{:S(2)}, u32[]{:S(2)}) %collective-permute-start.14) | collective-permute-done | bytes 131104 | tf_op jit(solution)/shard_map/ppermute | solution.py:20
  40.5 1.3 %collective-permute-start.15 = (bf16[16,4096]{1,0:T(8,128)(2,1)S(1)}, bf16[16,4096]{1,0:T(8,128)(2,1)S(1)}, u32[]{:S(2)}, u32[]{:S(2)}) collective-permute-start(bf16[16,4096]{1,0:T(8,128)(2,1)S(1)} %pair.3), channel_id=1, source_target_pairs={{0,8},{4,12},{8,0},{12,4},{16,24},{20,28},{24,16},{28,20},{1,9},{5... | collective-permute-start | bytes 393224 | tf_op jit(solution)/shard_map/ppermute | solution.py:20
  41.9 0.9 %collective-permute-start.16 = (bf16[16,4096]{1,0:T(8,128)(2,1)S(1)}, bf16[16,4096]{1,0:T(8,128)(2,1)S(1)}, u32[]{:S(2)}, u32[]{:S(2)}) collective-permute-start(bf16[16,4096]{1,0:T(8,128)(2,1)S(1)} %get-tuple-element.31), channel_id=1, source_target_pairs={{0,16},{4,20},{8,24},{12,28},{16,0},{20,4},{24,8},{28,12},{1,17},{... | collective-permute-start | bytes 393224 | tf_op jit(solution)/shard_map/ppermute | solution.py:20
  42.8 1.4 %collective-permute-start.17 = (bf16[16,4096]{1,0:T(8,128)(2,1)S(1)}, bf16[16,4096]{1,0:T(8,128)(2,1)S(1)}, u32[]{:S(2)}, u32[]{:S(2)}) collective-permute-start(bf16[16,4096]{1,0:T(8,128)(2,1)S(1)} %get-tuple-element.32), channel_id=1, source_target_pairs={{0,24},{4,28},{8,16},{12,20},{16,8},{20,12},{24,0},{28,4},{1,25},{... | collective-permute-start | bytes 393224 | tf_op jit(solution)/shard_map/ppermute | solution.py:20
  44.8 1.9 %collective-permute-done.15.refs_0_ = bf16[16,4096]{1,0:T(8,128)(2,1)S(1)} collective-permute-done((bf16[16,4096]{1,0:T(8,128)(2,1)S(1)}, bf16[16,4096]{1,0:T(8,128)(2,1)S(1)}, u32[]{:S(2)}, u32[]{:S(2)}) %collective-permute-start.15) | collective-permute-done | bytes 131104 | tf_op jit(solution)/shard_map/ppermute | solution.py:20
  46.7 3.3 %collective-permute-done.16.refs_1_ = bf16[16,4096]{1,0:T(8,128)(2,1)S(1)} collective-permute-done((bf16[16,4096]{1,0:T(8,128)(2,1)S(1)}, bf16[16,4096]{1,0:T(8,128)(2,1)S(1)}, u32[]{:S(2)}, u32[]{:S(2)}) %collective-permute-start.16) | collective-permute-done | bytes 131104 | tf_op jit(solution)/shard_map/ppermute | solution.py:20
  50.0 0.7 %final.1 = f32[16,4096]{1,0:T(8,128)} custom-call(f32[16,4096]{1,0:T(8,128)S(1)} %get-tuple-element.29.own, bf16[16,4096]{1,0:T(8,128)(2,1)S(1)} %collective-permute-done.15.refs_0_, bf16[16,4096]{1,0:T(8,128)(2,1)S(1)} %collective-permute-done.16.refs_1_, bf16[16,4096]{1,0:T(8,128)(2,1)S(1)} %collective-permute-done.17.refs_2_), custom_call_target="tpu_custom_call" | custom-call | flops 196608 | bytes 786432 | tf_op jit(solution)/shard_map/final/pallas_call | solution.py:319
  (25 shorter events, 3.0 us)
Async XLA Ops:
  0.6 7.2 %collective-permute-start = (bf16[16,4096]{1,0:T(8,128)(2,1)}, bf16[16,4096]{1,0:T(8,128)(2,1)S(1)}, u32[]{:S(2)}, u32[]{:S(2)}) collective-permute-start(bf16[16,4096]{1,0:T(8,128)(2,1)} %refs_1_.1), channel_id=1, source_target_pairs={{0,8},{4,12},{8,0},{12,4},{16,24},{20,28},{24,16},{28,20},{1,9},{5... | collective-permute-start | bytes 393224 | tf_op jit(solution)/shard_map/ppermute | solution.py:20
  3.7 8.0 %collective-permute-start.3 = (bf16[16,4096]{1,0:T(8,128)(2,1)}, bf16[16,4096]{1,0:T(8,128)(2,1)S(1)}, u32[]{:S(2)}, u32[]{:S(2)}) collective-permute-start(bf16[16,4096]{1,0:T(8,128)(2,1)} %refs_1_.1), channel_id=1, source_target_pairs={{0,16},{4,20},{8,24},{12,28},{16,0},{20,4},{24,8},{28,12},{1,17},{... | collective-permute-start | bytes 393224 | tf_op jit(solution)/shard_map/ppermute | solution.py:20
  5.2 6.5 %collective-permute-start.5 = (bf16[16,4096]{1,0:T(8,128)(2,1)}, bf16[16,4096]{1,0:T(8,128)(2,1)S(1)}, u32[]{:S(2)}, u32[]{:S(2)}) collective-permute-start(bf16[16,4096]{1,0:T(8,128)(2,1)} %refs_1_.1), channel_id=1, source_target_pairs={{0,24},{4,28},{8,16},{12,20},{16,8},{20,12},{24,0},{28,4},{1,25},{... | collective-permute-start | bytes 393224 | tf_op jit(solution)/shard_map/ppermute | solution.py:20
  5.2 11.7 %collective-permute-start.2 = (bf16[16,4096]{1,0:T(8,128)(2,1)}, bf16[16,4096]{1,0:T(8,128)(2,1)S(1)}, u32[]{:S(2)}, u32[]{:S(2)}) collective-permute-start(bf16[16,4096]{1,0:T(8,128)(2,1)} %refs_1_.1), channel_id=1, source_target_pairs={{0,4},{4,0},{8,12},{12,8},{16,20},{20,16},{24,28},{28,24},{1,5},{5... | collective-permute-start | bytes 393224 | tf_op jit(solution)/shard_map/ppermute | solution.py:20
  7.9 9.1 %collective-permute-start.1 = (bf16[16,4096]{1,0:T(8,128)(2,1)S(1)}, bf16[16,4096]{1,0:T(8,128)(2,1)S(1)}, u32[]{:S(2)}, u32[]{:S(2)}) collective-permute-start(bf16[16,4096]{1,0:T(8,128)(2,1)S(1)} %collective-permute-done.refs_0_), channel_id=1, source_target_pairs={{0,4},{4,0},{8,12},{12,8},{16,20},{20,16},{24,28},{28,24},{1,5},{5... | collective-permute-start | bytes 393224 | tf_op jit(solution)/shard_map/ppermute | solution.py:20
  11.7 5.3 %collective-permute-start.4 = (bf16[16,4096]{1,0:T(8,128)(2,1)S(1)}, bf16[16,4096]{1,0:T(8,128)(2,1)S(1)}, u32[]{:S(2)}, u32[]{:S(2)}) collective-permute-start(bf16[16,4096]{1,0:T(8,128)(2,1)S(1)} %collective-permute-done.3.refs_2_), channel_id=1, source_target_pairs={{0,4},{4,0},{8,12},{12,8},{16,20},{20,16},{24,28},{28,24},{1,5},{5... | collective-permute-start | bytes 393224 | tf_op jit(solution)/shard_map/ppermute | solution.py:20
  11.7 5.3 %collective-permute-start.6 = (bf16[16,4096]{1,0:T(8,128)(2,1)S(1)}, bf16[16,4096]{1,0:T(8,128)(2,1)S(1)}, u32[]{:S(2)}, u32[]{:S(2)}) collective-permute-start(bf16[16,4096]{1,0:T(8,128)(2,1)S(1)} %collective-permute-done.5.refs_3_), channel_id=1, source_target_pairs={{0,4},{4,0},{8,12},{12,8},{16,20},{20,16},{24,28},{28,24},{1,5},{5... | collective-permute-start | bytes 393224 | tf_op jit(solution)/shard_map/ppermute | solution.py:20
  12.2 4.6 %copy-start = (bf16[16,4096]{1,0:T(8,128)(2,1)S(1)}, bf16[16,4096]{1,0:T(8,128)(2,1)}, u32[]{:S(2)}) copy-start(bf16[16,4096]{1,0:T(8,128)(2,1)} %refs_1_.1) | copy-start | bytes 393220
  19.0 5.9 %collective-permute-start.9 = (f32[128,128]{1,0:T(8,128)S(1)}, f32[128,128]{1,0:T(8,128)S(1)}, u32[]{:S(2)}, u32[]{:S(2)}) collective-permute-start(f32[128,128]{1,0:T(8,128)S(1)} %own_score.3), channel_id=1, source_target_pairs={{0,1},{1,0},{2,3},{3,2},{4,5},{5,4},{6,7},{7,6},{8,9},{9,8},{10,11... | collective-permute-start | bytes 196616 | tf_op jit(solution)/shard_map/ppermute | solution.py:20
  20.7 7.5 %collective-permute-start.7 = (f32[128,128]{1,0:T(8,128)S(1)}, f32[128,128]{1,0:T(8,128)S(1)}, u32[]{:S(2)}, u32[]{:S(2)}) collective-permute-start(f32[128,128]{1,0:T(8,128)S(1)} %get-tuple-element.24), channel_id=1, source_target_pairs={{0,2},{1,3},{2,0},{3,1},{4,6},{5,7},{6,4},{7,5},{8,10},{9,11},{10,... | collective-permute-start | bytes 196616 | tf_op jit(solution)/shard_map/ppermute | solution.py:20
  23.3 6.2 %collective-permute-start.8 = (f32[128,128]{1,0:T(8,128)S(1)}, f32[128,128]{1,0:T(8,128)S(1)}, u32[]{:S(2)}, u32[]{:S(2)}) collective-permute-start(f32[128,128]{1,0:T(8,128)S(1)} %get-tuple-element.25), channel_id=1, source_target_pairs={{0,3},{1,2},{2,1},{3,0},{4,7},{5,6},{6,5},{7,4},{8,11},{9,10},{10,... | collective-permute-start | bytes 196616 | tf_op jit(solution)/shard_map/ppermute | solution.py:20
  29.5 4.5 %collective-permute-start.10 = (bf16[144,128]{1,0:T(8,128)(2,1)S(1)}, bf16[144,128]{1,0:T(8,128)(2,1)S(1)}, u32[]{:S(2)}, u32[]{:S(2)}) collective-permute-start(bf16[144,128]{1,0:T(8,128)(2,1)S(1)} %weigh.1.refs_0_), channel_id=1, source_target_pairs={{0,1},{1,0},{2,3},{3,2},{4,5},{5,4},{6,7},{7,6},{8,9},{9,8},{10,11... | collective-permute-start | bytes 110600 | tf_op jit(solution)/shard_map/ppermute | solution.py:20
  30.3 4.9 %collective-permute-start.11 = (bf16[144,128]{1,0:T(8,128)(2,1)S(1)}, bf16[144,128]{1,0:T(8,128)(2,1)S(1)}, u32[]{:S(2)}, u32[]{:S(2)}) collective-permute-start(bf16[144,128]{1,0:T(8,128)(2,1)S(1)} %weigh.1.refs_0_), channel_id=1, source_target_pairs={{0,2},{1,3},{2,0},{3,1},{4,6},{5,7},{6,4},{7,5},{8,10},{9,11},{10,... | collective-permute-start | bytes 110600 | tf_op jit(solution)/shard_map/ppermute | solution.py:20
  32.0 5.8 %collective-permute-start.12 = (bf16[144,128]{1,0:T(8,128)(2,1)S(1)}, bf16[144,128]{1,0:T(8,128)(2,1)S(1)}, u32[]{:S(2)}, u32[]{:S(2)}) collective-permute-start(bf16[144,128]{1,0:T(8,128)(2,1)S(1)} %weigh.1.refs_0_), channel_id=1, source_target_pairs={{0,3},{1,2},{2,1},{3,0},{4,7},{5,6},{6,5},{7,4},{8,11},{9,10},{10,... | collective-permute-start | bytes 110600 | tf_op jit(solution)/shard_map/ppermute | solution.py:20
  38.5 3.3 %collective-permute-start.13 = (bf16[48,4096]{1,0:T(8,128)(2,1)S(1)}, bf16[48,4096]{1,0:T(8,128)(2,1)S(1)}, u32[]{:S(2)}, u32[]{:S(2)}) collective-permute-start(bf16[48,4096]{1,0:T(8,128)(2,1)S(1)} %get-tuple-element.28), channel_id=1, source_target_pairs={{0,4},{4,0},{8,12},{12,8},{16,20},{20,16},{24,28},{28,24},{1,5},{5... | collective-permute-start | bytes 1179656 | tf_op jit(solution)/shard_map/ppermute | solution.py:20
  38.6 1.9 %collective-permute-start.14 = (bf16[16,4096]{1,0:T(8,128)(2,1)S(1)}, bf16[16,4096]{1,0:T(8,128)(2,1)S(1)}, u32[]{:S(2)}, u32[]{:S(2)}) collective-permute-start(bf16[16,4096]{1,0:T(8,128)(2,1)S(1)} %get-tuple-element.30), channel_id=1, source_target_pairs={{0,4},{4,0},{8,12},{12,8},{16,20},{20,16},{24,28},{28,24},{1,5},{5... | collective-permute-start | bytes 393224 | tf_op jit(solution)/shard_map/ppermute | solution.py:20
  40.5 6.2 %collective-permute-start.15 = (bf16[16,4096]{1,0:T(8,128)(2,1)S(1)}, bf16[16,4096]{1,0:T(8,128)(2,1)S(1)}, u32[]{:S(2)}, u32[]{:S(2)}) collective-permute-start(bf16[16,4096]{1,0:T(8,128)(2,1)S(1)} %pair.3), channel_id=1, source_target_pairs={{0,8},{4,12},{8,0},{12,4},{16,24},{20,28},{24,16},{28,20},{1,9},{5... | collective-permute-start | bytes 393224 | tf_op jit(solution)/shard_map/ppermute | solution.py:20
  41.9 8.1 %collective-permute-start.16 = (bf16[16,4096]{1,0:T(8,128)(2,1)S(1)}, bf16[16,4096]{1,0:T(8,128)(2,1)S(1)}, u32[]{:S(2)}, u32[]{:S(2)}) collective-permute-start(bf16[16,4096]{1,0:T(8,128)(2,1)S(1)} %get-tuple-element.31), channel_id=1, source_target_pairs={{0,16},{4,20},{8,24},{12,28},{16,0},{20,4},{24,8},{28,12},{1,17},{... | collective-permute-start | bytes 393224 | tf_op jit(solution)/shard_map/ppermute | solution.py:20
  42.8 7.2 %collective-permute-start.17 = (bf16[16,4096]{1,0:T(8,128)(2,1)S(1)}, bf16[16,4096]{1,0:T(8,128)(2,1)S(1)}, u32[]{:S(2)}, u32[]{:S(2)}) collective-permute-start(bf16[16,4096]{1,0:T(8,128)(2,1)S(1)} %get-tuple-element.32), channel_id=1, source_target_pairs={{0,24},{4,28},{8,16},{12,20},{16,8},{20,12},{24,0},{28,4},{1,25},{... | collective-permute-start | bytes 393224 | tf_op jit(solution)/shard_map/ppermute | solution.py:20
